TPU v7x, 32 devices: a whole 2x2x4 slice. The times are simulated.
32 devices in a mesh: section: 2 (over core), dp: 16 (over z, y, x).
Axes of the slice: x: 2, y: 2, z: 4, core: 2. Of those that a mesh axis runs over, the one named last changes fastest.
Arguments:
- replay: bfloat16 [2048, 4096], P('dp'), may hold values from -6 to 6
- state_ids: int32 [2048], P('dp'), may hold values from 0 to 2047, as said below
- sampled: int32 [2048, 20], P('dp'), may hold values from 0 to 255
- targets: int32 [2048], P('dp'), may hold values from 0 to 19
- action_table: bfloat16 [256, 4096], replicated, may hold values from -6 to 6
- norm_gain: float32 [2, 4096], P('section'), may hold values from 0.5 to 1.5
- w_up: bfloat16 [2, 4096, 512], P('section', 'dp'), may hold values from -0.09375 to 0.09375
- w_down: bfloat16 [2, 512, 4096], P('section', 'dp'), may hold values from -0.25 to 0.25
Outputs:
- grad_up: float32 [2, 4096, 512], P('section', 'dp')
- grad_down: float32 [2, 512, 4096], P('section', 'dp')
- grad_gain: float32 [2, 4096], P('section')
- loss: float32 [], replicated
Inputs may be any that keep to these rules, and one draw needn't show every extreme that they name: state_ids[i] // 128 == i // 128: a state's replay row lies in the same aligned block of 128 rows as the state.
All inputs are finite; a program needn't handle non-finite values.
Results may differ from a plain program's by a relative error of at most 0.011.
Values may be sent and summed in bfloat16 or wider, within the bound.
A program may use at most 128 MiB of HBM per device.

v0:
```python
import functools
import math

import jax
import jax.numpy as jnp
from jax import lax
from jax.experimental import pallas as pl
from jax.experimental.pallas import tpu as pltpu
from jax.sharding import PartitionSpec as P

ROWS_DEV = 128
epsilon = 1e-06
logit_cap = 15.0
bf16 = jnp.bfloat16
f32 = jnp.float32


def contract_last(left, right):
    return lax.dot_general(left, right, (((1,), (1,)), ((), ())), preferred_element_type=f32)


def contract_first(left, right):
    return lax.dot_general(left, right, (((0,), (0,)), ((), ())), preferred_element_type=f32)


def dot(left, right):
    return jnp.dot(left, right, preferred_element_type=f32)


def spread(rows, column, axis):
    here = lax.broadcasted_iota(jnp.int32, (rows, rows), 0)
    there = lax.broadcasted_iota(jnp.int32, (rows, rows), 1)
    wide = jnp.broadcast_to(column, (rows, rows))
    return jnp.sum(jnp.where(here == there, wide, 0.0), axis, keepdims=True)


class Group:
    def __init__(self, size, me, target):
        self.size, self.me, self.target = size, me, target

    def copy(self, k, source, dest, send_sem, recv_sem):
        peer = lax.rem(self.me + k, self.size)
        made = pltpu.make_async_remote_copy(
            src_ref=source(peer),
            dst_ref=dest,
            send_sem=send_sem,
            recv_sem=recv_sem,
            device_id=self.target(peer),
            device_id_type=pl.DeviceIdType.MESH,
        )
        made.start()
        return made

    def fan(self, source, dest, sems):
        return [
            self.copy(k, source, dest, sems.at[0, k], sems.at[1, k])
            for k in range(1, self.size)
        ]


def groups_of(outer, inner, sections):
    pos = lax.axis_index("dp")
    high, low = lax.div(pos, inner), lax.rem(pos, inner)
    return (
        Group(outer, high, lambda p: {"dp": p * inner + low}),
        Group(inner, low, lambda p: {"dp": pos - low + p}),
        Group(sections, lax.axis_index("section"), lambda p: {"section": p}),
    )


def greet(*groups):
    barrier = pltpu.get_barrier_semaphore()
    for group in groups:
        for k in range(1, group.size):
            pl.semaphore_signal(
                barrier,
                inc=1,
                device_id=group.target(lax.rem(group.me + k, group.size)),
                device_id_type=pl.DeviceIdType.MESH,
            )
    pl.semaphore_wait(barrier, sum(group.size - 1 for group in groups))


def local(source, dest, sem):
    made = pltpu.make_async_copy(source, dest, sem)
    made.start()
    return made


def land(copies):
    for copy in copies:
        copy.wait_recv()


def drain(copies):
    for copy in copies:
        copy.wait_send()


def stage_kernel(dims, start, down, up, gain, state, ups, downs, gains, sems, pass_sems, own_sems):
    across, within, between = groups_of(*dims)
    z, j, s = across.me, within.me, between.me
    greet(across, within, between)
    down_cuts = across.fan(lambda p: down.at[p], downs.at[s, z, j], sems.at[0])
    up_rows = within.fan(lambda p: up, ups.at[s, j], sems.at[1])
    states = across.fan(lambda p: start.at[p], state.at[z], sems.at[2])
    sent = between.fan(lambda p: gain, gains.at[s], sems.at[3])
    sent += between.fan(lambda p: up, ups.at[s, j], pass_sems.at[0, 0])
    down_own = local(down.at[z], downs.at[s, z, j], own_sems.at[0])
    own = [
        local(up, ups.at[s, j], own_sems.at[1]),
        local(start.at[z], state.at[z], own_sems.at[2]),
        local(gain, gains.at[s], own_sems.at[3]),
    ]
    down_own.wait()
    land(down_cuts)
    mine = downs.at[s, :, j]
    down_rows = within.fan(lambda p: mine, mine, sems.at[4])
    sent += between.fan(lambda p: mine, mine, pass_sems.at[1, 0])
    for number, rows in ((0, up_rows), (1, down_rows)):
        for k in range(1, within.size):
            rows[k - 1].wait_recv()
            giver = lax.rem(j + within.size - k, within.size)
            piece = ups.at[s, giver] if number == 0 else downs.at[s, :, giver]
            sent += between.fan(lambda p: piece, piece, pass_sems.at[number, k])
    land(states + sent)
    drain(down_cuts + up_rows + states + down_rows + sent)
    for copy in own:
        copy.wait()


def forward_kernel(dims, width, first, parts, stat, upper, actives, recips, recip, got, stats, row, mine, sems, own_sems):
    across, _, _ = groups_of(*dims)
    z, size = across.me, across.size
    rows = upper.shape[0]
    greet(across)
    sent = across.fan(lambda p: parts.at[p], got.at[z], sems.at[0])
    if not first:
        sent += across.fan(lambda p: stat.at[p], stats.at[z], sems.at[1])
    own = local(parts.at[z], got.at[z], own_sems.at[0])
    own.wait()
    if not first:
        own_stat = local(stat.at[z], stats.at[z], own_sems.at[1])
        own_stat.wait()
    land(sent)
    if first:
        squares = stat[...]
    else:
        squares = spread(rows, jnp.sum(stats[...], 0), 1)
    factor = lax.rsqrt(squares / width + epsilon)
    recip[...] = factor
    total = jnp.sum(got[...].astype(f32), 0) * factor
    active = (total * jax.nn.sigmoid(total)).astype(bf16)
    mine[...] = active
    row[...] = spread(rows, factor, 0)
    upper[...] = total
    more = across.fan(lambda p: mine, actives.at[z], sems.at[2])
    more += across.fan(lambda p: row, recips.at[z], sems.at[3])
    ends = [
        local(mine, actives.at[z], own_sems.at[2]),
        local(row, recips.at[z], own_sems.at[3]),
    ]
    land(more)
    drain(sent + more)
    for copy in ends:
        copy.wait()


def backward_kernel(dims, width, parts, upper, recip, d_uppers, pulls, got, row, mine, sems, own_sems):
    across, _, _ = groups_of(*dims)
    z = across.me
    rows = upper.shape[0]
    greet(across)
    sent = across.fan(lambda p: parts.at[p], got.at[z], sems.at[0])
    own = local(parts.at[z], got.at[z], own_sems.at[0])
    value = upper[...]
    sigm = jax.nn.sigmoid(value)
    slope = sigm * (1.0 + value * (1.0 - sigm))
    own.wait()
    land(sent)
    d_upper = (jnp.sum(got[...].astype(f32), 0) * slope).astype(bf16)
    mine[...] = d_upper
    factor = recip[...]
    pull = jnp.sum(d_upper.astype(f32) * value, -1, keepdims=True) * factor * factor / width
    row[...] = spread(rows, pull, 0)
    more = across.fan(lambda p: mine, d_uppers.at[z], sems.at[1])
    more += across.fan(lambda p: row, pulls.at[z], sems.at[2])
    ends = [
        local(mine, d_uppers.at[z], own_sems.at[1]),
        local(row, pulls.at[z], own_sems.at[2]),
    ]
    land(more)
    drain(sent + more)
    for copy in ends:
        copy.wait()


def head_kernel(dims, scale, parts, picks, marks, grads, loss, got, mine, sems, own_sems):
    across, _, _ = groups_of(*dims)
    z = across.me
    rows, samples = picks.shape
    vocab = parts.shape[2]
    greet(across)
    sent = across.fan(lambda p: parts.at[p], got.at[z], sems.at[0])
    own = local(parts.at[z], got.at[z], own_sems.at[0])
    own.wait()
    land(sent)
    scores = jnp.sum(got[...], 0) / scale
    actions = lax.broadcasted_iota(jnp.int32, (rows, vocab), 1)
    choice = picks[...]
    chosen = jnp.concatenate(
        [
            jnp.sum(jnp.where(choice[:, k : k + 1] == actions, scores, 0.0), -1, keepdims=True)
            for k in range(samples)
        ],
        1,
    )
    bent = jnp.tanh(chosen / logit_cap)
    logits = logit_cap * bent
    expo = jnp.exp(logits)
    summed = jnp.sum(expo, -1, keepdims=True)
    order = lax.broadcasted_iota(jnp.int32, (rows, samples), 1)
    hot = jnp.where(marks[...] == order, 1.0, 0.0)
    cross = jnp.log(summed) - jnp.sum(logits * hot, -1, keepdims=True)
    loss[...] = jnp.broadcast_to(jnp.sum(cross, 0, keepdims=True) / ROWS_DEV, loss.shape)
    d_chosen = (expo / summed - hot) / ROWS_DEV * (1.0 - bent * bent) / scale
    d_scores = jnp.zeros((rows, vocab), f32)
    for k in range(samples):
        d_scores += jnp.where(choice[:, k : k + 1] == actions, d_chosen[:, k : k + 1], 0.0)
    mine[...] = d_scores.astype(bf16)
    more = across.fan(lambda p: mine, grads.at[z], sems.at[1])
    end = local(mine, grads.at[z], own_sems.at[1])
    land(more)
    drain(sent + more)
    end.wait()


def finish_kernel(
    dims, up, down, small, grad_up, down_out, small_out,
    up_got, down_got, small_got, up_sum, down_sum, small_sum,
    up_rows, down_rows, small_rows, down_full, small_full, sems, own_sems,
):
    across, within, between = groups_of(*dims)
    z, j, s = across.me, within.me, between.me
    greet(across, within, between)

    def total(mine, got, group):
        value = mine.astype(f32)
        for k in range(1, group.size):
            value += got[k - 1].astype(f32)
        return value

    def swap(group, source, got, sems):
        return [
            group.copy(k, source, got.at[k - 1], sems.at[0, k], sems.at[1, k])
            for k in range(1, group.size)
        ]

    downs = swap(between, lambda p: down.at[p], down_got, sems.at[0])
    ups = swap(between, lambda p: up.at[p], up_got, sems.at[1])
    smalls = swap(between, lambda p: small.at[p], small_got, sems.at[2])
    land(downs)
    for part in range(across.size):
        value = down[s, part].astype(f32)
        for k in range(1, between.size):
            value += down_got[k - 1, part].astype(f32)
        down_sum[part] = value.astype(bf16)
    down_in = swap(within, lambda p: down_sum.at[:, p], down_rows, sems.at[3])
    land(smalls)
    small_sum[...] = total(small[s], small_got, between)
    small_in = swap(within, lambda p: small_sum, small_rows, sems.at[4])
    land(ups)
    for part in range(within.size):
        value = up[s, part].astype(f32)
        for k in range(1, between.size):
            value += up_got[k - 1, part].astype(f32)
        up_sum[part] = value.astype(bf16)
    up_in = swap(within, lambda p: up_sum.at[p], up_rows, sems.at[5])
    land(down_in)
    down_full[...] = total(down_sum[:, j], down_rows, within).astype(bf16)
    down_ends = across.fan(lambda p: down_full.at[p], down_out.at[z], sems.at[6])
    land(small_in)
    small_full[...] = total(small_sum[...], small_rows, within)
    small_ends = across.fan(lambda p: small_full, small_out.at[z], sems.at[7])
    own = [
        local(down_full.at[z], down_out.at[z], own_sems.at[0]),
        local(small_full, small_out.at[z], own_sems.at[1]),
    ]
    land(up_in)
    grad_up[...] = total(up_sum[j], up_rows, within)
    land(down_ends + small_ends)
    drain(downs + ups + smalls + down_in + small_in + up_in + down_ends + small_ends)
    for copy in own:
        copy.wait()


def call(ident, kernel, args, outs, scratch, sem_shapes):
    spec = pl.BlockSpec(memory_space=pltpu.VMEM)
    return pl.pallas_call(
        kernel,
        out_shape=[jax.ShapeDtypeStruct(shape, kind) for shape, kind in outs],
        in_specs=[spec] * len(args),
        out_specs=[spec] * len(outs),
        scratch_shapes=[pltpu.VMEM(shape, kind) for shape, kind in scratch]
        + [pltpu.SemaphoreType.DMA(shape) for shape in sem_shapes],
        compiler_params=pltpu.CompilerParams(collective_id=ident, has_side_effects=True),
    )(*args)


def on_device(replay, state_ids, sampled, targets, action_table, norm_gain, w_up, w_down):
    sections = lax.axis_size("section")
    devices = lax.axis_size("dp")
    outer = 1
    while outer * outer < devices:
        outer *= 2
    inner = devices // outer
    dims = (outer, inner, sections)
    top = max(dims)
    section_pos = lax.axis_index("section")
    dp_pos = lax.axis_index("dp")
    outer_pos = dp_pos // inner
    held_rows, width = replay.shape
    rows = held_rows // sections
    vocab = action_table.shape[0]
    cut = width // outer
    ff = w_up.shape[2]
    up_held = w_up.shape[1]
    ff_held = w_down.shape[1]
    group_rows = outer * rows
    scale = math.sqrt(width)
    small_width = cut + 128

    def my_rows(x):
        return lax.dynamic_slice_in_dim(x, section_pos * rows, rows, 0)

    def my_cut(x):
        return lax.dynamic_slice_in_dim(x, outer_pos * cut, cut, 1)

    def to_cuts(x):
        return x.reshape(x.shape[0], outer, cut).transpose(1, 0, 2)

    ids = my_rows(state_ids) - dp_pos * held_rows
    picks = my_rows(sampled)
    marks = my_rows(targets)
    table_cut = my_cut(action_table)
    id_hot = (ids[:, None] == jnp.arange(held_rows)[None, :]).astype(bf16)
    taken_hot = (picks[:, 0:1] == jnp.arange(vocab)[None, :]).astype(bf16)
    start = (dot(id_hot, replay) + dot(taken_hot, action_table)).astype(bf16)
    start_wide = start.astype(f32)
    squares = jnp.sum(start_wide * start_wide, -1, keepdims=True)

    state_cuts, ups, downs, gains = call(
        0,
        functools.partial(stage_kernel, dims),
        (to_cuts(start), to_cuts(w_down[0]), w_up[0], my_cut(norm_gain)),
        (
            ((outer, rows, cut), bf16),
            ((sections, inner, up_held, ff), bf16),
            ((sections, outer, inner, ff_held, cut), bf16),
            ((sections, 1, cut), f32),
        ),
        (),
        ((5, 2, top), (2, inner, 2, top), (4,)),
    )
    ups = ups.reshape(sections, cut, ff)
    downs = downs.reshape(sections, ff, cut)

    state = state_cuts.reshape(group_rows, cut)
    kept = []
    for layer in range(sections):
        wide = state.astype(f32)
        part = dot((wide * gains[layer]).astype(bf16), ups[layer]).astype(bf16)
        first = layer == 0
        stat = squares if first else jnp.sum(wide * wide, -1).reshape(outer, 1, rows)
        upper, actives, recips, recip = call(
            1 + layer,
            functools.partial(forward_kernel, dims, width, first),
            (part.reshape(outer, rows, ff), stat),
            (
                ((rows, ff), f32),
                ((outer, rows, ff), bf16),
                ((outer, 1, rows), f32),
                ((rows, 1), f32),
            ),
            (
                ((outer, rows, ff), bf16),
                ((outer, 1, rows), f32),
                ((1, rows), f32),
                ((rows, ff), bf16),
            ),
            ((4, 2, top), (4,)),
        )
        actives = actives.reshape(group_rows, ff)
        kept.append((state, recip, upper, actives, recips.reshape(group_rows, 1)))
        state = (wide + dot(actives, downs[layer])).astype(bf16)

    score_part = contract_last(state, table_cut).reshape(outer, rows, vocab)
    d_all, loss_row = call(
        1 + sections,
        functools.partial(head_kernel, dims, scale),
        (score_part, picks, marks[:, None]),
        (((outer, rows, vocab), bf16), ((1, 128), f32)),
        (((outer, rows, vocab), f32), ((rows, vocab), bf16)),
        ((2, 2, top), (2,)),
    )
    grad = dot(d_all.reshape(group_rows, vocab), table_cut).astype(bf16)

    grads_up, grads_down, grads_gain = [], [], []
    for layer in reversed(range(sections)):
        state, recip, upper, actives, recips = kept[layer]
        part = contract_last(grad, downs[layer]).astype(bf16).reshape(outer, rows, ff)
        d_uppers, pulls = call(
            2 + sections + layer,
            functools.partial(backward_kernel, dims, width),
            (part, upper, recip),
            (((outer, rows, ff), bf16), ((outer, 1, rows), f32)),
            (((outer, rows, ff), bf16), ((1, rows), f32), ((rows, ff), bf16)),
            ((3, 2, top), (3,)),
        )
        d_uppers = d_uppers.reshape(group_rows, ff)
        pulls = pulls.reshape(group_rows, 1)
        wide = state.astype(f32)
        ready = wide * recips
        d_normed = contract_last(d_uppers, ups[layer])
        grads_gain.append(jnp.sum(d_normed * ready, 0))
        normed = (ready * gains[layer]).astype(bf16)
        grads_up.append(contract_first(normed, d_uppers).astype(bf16))
        grads_down.append(contract_first(actives, grad).astype(bf16))
        if layer:
            grad = (
                grad.astype(f32) + d_normed * gains[layer] * recips - wide * pulls
            ).astype(bf16)

    gain_rows = jnp.stack(grads_gain[::-1])[:, None, :]
    loss_rows = jnp.broadcast_to(loss_row, (sections, 1, 128))
    small = jnp.concatenate([gain_rows, loss_rows], -1)
    others = sections - 1
    grad_up, down_got, small_got = call(
        2 + 2 * sections,
        functools.partial(finish_kernel, dims),
        (
            jnp.stack(grads_up[::-1]).reshape(sections, inner, up_held, ff),
            jnp.stack(grads_down[::-1]).reshape(sections, outer, inner, ff_held, cut),
            small,
        ),
        (
            ((up_held, ff), f32),
            ((outer, ff_held, cut), bf16),
            ((outer, 1, small_width), f32),
        ),
        (
            ((others, inner, up_held, ff), bf16),
            ((others, outer, inner, ff_held, cut), bf16),
            ((others, 1, small_width), f32),
            ((inner, up_held, ff), bf16),
            ((outer, inner, ff_held, cut), bf16),
            ((1, small_width), f32),
            ((inner - 1, up_held, ff), bf16),
            ((inner - 1, outer, ff_held, cut), bf16),
            ((inner - 1, 1, small_width), f32),
            ((outer, ff_held, cut), bf16),
            ((1, small_width), f32),
        ),
        ((8, 2, top), (2,)),
    )
    grad_down = down_got.transpose(1, 0, 2).reshape(ff_held, width).astype(f32)
    grad_gain = small_got[:, 0, :cut].reshape(1, width)
    loss = jnp.sum(small_got[:, 0, cut])
    return (grad_up[None], grad_down[None], grad_gain, loss)


def solution(mesh):
    return jax.shard_map(
        on_device,
        mesh=mesh,
        in_specs=(
            P("dp", None),
            P("dp"),
            P("dp", None),
            P("dp"),
            P(),
            P("section", None),
            P("section", "dp", None),
            P("section", "dp", None),
        ),
        out_specs=(P("section", "dp", None), P("section", "dp", None), P("section", None), P()),
        check_vma=False,
    )
```

profile of v0, /device:TPU:0, one launch (start us, length us, event | category | flops | bytes accessed | tf_op | source)
XLA Modules:
  0.0 198.3 jit_solution(17301103993843523532)
XLA Ops:
  1.5 1.6 fusion.23
  5.9 1.3 constant_dynamic-slice_fusion.gain
  7.2 35.3 %shard_map.111 = (bf16[4,64,1024]{2,1,0:T(8,128)(2,1)}, bf16[2,4,256,512]{3,2,1,0:T(8,128)(2,1)}, bf16[2,4,4,32,1024]{4,3,2,1,0:T(8,128)(2,1)}, f32[2,1,1024]{2,1,0:T(1,128)}) custom-call(bf16[4,64,1024]{2,1,0:T(8,128)(2,1)} %bitcast.81, bf16[4,32,1024]{2,1,0:T(8,128)(2,1)} %bitcast.87, bf16[256,512]{1,0:T(8,128)(2,1)} %bitcast.100, ...), custom_call_target="tpu_custom_call" | custom-call | tf_op jit(solution)/shard_map/pallas_call | solution.py:299
  42.5 2.8 %fusion.28 = (bf16[1,4,256,512]{3,2,1,0:T(8,128)(2,1)S(1)}, bf16[1,4,256,512]{3,2,1,0:T(8,128)(2,1)}) fusion(bf16[2,4,256,512]{3,2,1,0:T(8,128)(2,1)} %get-tuple-element.26), kind=kLoop, calls=%fused_computation.62 | loop fusion | bytes 4194304 | tf_op jit(solution)/shard_map/slice | solution.py:372
  47.2 17.8 %shard_map.112 = (f32[64,512]{1,0:T(8,128)}, bf16[4,64,512]{2,1,0:T(8,128)(2,1)}, f32[4,1,64]{2,1,0:T(1,128)}, f32[64,1]{1,0:T(8,128)}) custom-call(bf16[4,64,512]{2,1,0:T(8,128)(2,1)} %bitcast.84, f32[64,1]{1,0:T(8,128)} %copy.18.stat), custom_call_target="tpu_custom_call" | custom-call | tf_op jit(solution)/shard_map/pallas_call | solution.py:299
  65.1 2.8 %fusion.27 = (bf16[1,4,4,32,1024]{4,3,2,1,0:T(8,128)(2,1)}, bf16[1,4,4,32,1024]{4,3,2,1,0:T(8,128)(2,1)S(1)}) fusion(bf16[2,4,4,32,1024]{4,3,2,1,0:T(8,128)(2,1)} %get-tuple-element.29), kind=kLoop, calls=%fused_computation.61 | loop fusion | bytes 4194304 | tf_op jit(solution)/shard_map/slice | solution.py:395
  68.4 1.2 copy-done.9
  69.7 1.2 convolution_convert_fusion.6
  71.5 15.9 %shard_map.113 = (f32[64,512]{1,0:T(8,128)}, bf16[4,64,512]{2,1,0:T(8,128)(2,1)}, f32[4,1,64]{2,1,0:T(1,128)}, f32[64,1]{1,0:T(8,128)}) custom-call(bf16[4,64,512]{2,1,0:T(8,128)(2,1)} %bitcast.99, f32[4,1,64]{2,1,0:T(1,128)} %reshape.111.stat), custom_call_target="tpu_custom_call" | custom-call | tf_op jit(solution)/shard_map/pallas_call | solution.py:299
  87.4 2.8 %fusion.6 = f32[256,256]{1,0:T(8,128)} fusion(bf16[256,512]{1,0:T(8,128)(2,1)} %bitcast.95, bf16[512,1024]{1,0:T(8,128)(2,1)} %bitcast.76, bf16[256,1024]{1,0:T(8,128)(2,1)} %copy-done.24, bf16[256,4096]{1,0:T(8,128)(2,1)S(1)} %copy-done, s32[]{:T(128)S(6)} %select_n.16), kind=kOutput, calls=%fused_computation.21 | convolution fusion | flops 403439616 | bytes 2621444 | tf_op jit(solution)/shard_map/dot_general | solution.py:19
  91.0 16.7 %shard_map.114 = (bf16[4,64,256]{2,1,0:T(8,128)(2,1)}, f32[1,128]{1,0:T(1,128)}) custom-call(f32[4,64,256]{2,1,0:T(8,128)} %bitcast.98, s32[64,20]{1,0:T(8,128)} %copy-done.12, s32[64,1]{1,0:T(8,128)} %copy.19.marks), custom_call_target="tpu_custom_call" | custom-call | tf_op jit(solution)/shard_map/pallas_call | solution.py:299
  107.7 1.2 convolution_convert_fusion.3
  109.8 2.4 %convolution_convert_fusion.5 = bf16[256,512]{1,0:T(8,128)(2,1)} fusion(bf16[256,1024]{1,0:T(8,128)(2,1)S(1)} %convolution_convert_fusion.3, bf16[512,1024]{1,0:T(8,128)(2,1)} %bitcast.77), kind=kOutput, calls=%fused_computation.23 | convolution fusion | flops 268566528 | bytes 1835008 | tf_op jit(solution)/shard_map/dot_general | solution.py:19
  112.2 17.6 %shard_map.115 = (bf16[4,64,512]{2,1,0:T(8,128)(2,1)}, f32[4,1,64]{2,1,0:T(1,128)}) custom-call(bf16[4,64,512]{2,1,0:T(8,128)(2,1)} %bitcast.85, f32[64,512]{1,0:T(8,128)} %get-tuple-element.32.upper, f32[64,1]{1,0:T(8,128)} %get-tuple-element.33.recip), custom_call_target="tpu_custom_call" | custom-call | tf_op jit(solution)/shard_map/pallas_call | solution.py:299
  131.0 2.7 %convolution_convert_fusion.2 = bf16[1024,512]{1,0:T(8,128)(2,1)} fusion(bf16[256,512]{1,0:T(8,128)(2,1)} %bitcast.113, bf16[256,1024]{1,0:T(8,128)(2,1)} %copy-done.24, f32[256]{0:T(256)S(1)} %mul.123, f32[1024]{0:T(1024)S(1)} %bitcast.107), kind=kOutput, calls=%fused_computation.12 | convolution fusion | flops 270008320 | bytes 1840128 | tf_op jit(solution)/shard_map/dot_general | solution.py:23
  133.7 1.3 reduce.13
  135.1 2.3 %fusion.8 = (f32[1024]{0:T(1024)S(1)}, bf16[256,1024]{1,0:T(8,128)(2,1)S(1)}) fusion(bf16[256,1024]{1,0:T(8,128)(2,1)} %copy-done.24, f32[256]{0:T(256)S(1)} %mul.123, f32[256]{0:T(256)S(1)} %mul.126, f32[1024]{0:T(1024)S(1)} %bitcast.108, bf16[256,1024]{1,0:T(8,128)(2,1)} %copy-done.1, bf16[256,512]{1,0:T(8,128)(2,1)} %bitcast.114, ...), kind=kOutput, calls=%fused_computation.27 | convolution fusion | flops 271318016 | bytes 2893824 | tf_op jit(solution)/shard_map/dot_general | solution.py:19
  137.5 1.2 convolution_convert_fusion.4
  138.7 15.5 %shard_map.116 = (bf16[4,64,512]{2,1,0:T(8,128)(2,1)}, f32[4,1,64]{2,1,0:T(1,128)}) custom-call(bf16[4,64,512]{2,1,0:T(8,128)(2,1)} %bitcast.86, f32[64,512]{1,0:T(8,128)} %get-tuple-element.37.upper, f32[64,1]{1,0:T(8,128)} %get-tuple-element.38.recip), custom_call_target="tpu_custom_call" | custom-call | tf_op jit(solution)/shard_map/pallas_call | solution.py:299
  154.2 1.7 bitcast_convert_fusion
  156.0 1.5 pad_maximum_fusion.up
  158.5 1.5 pad_maximum_fusion.1.down
  160.7 1.2 bitcast_multiply_fusion
  163.1 30.6 %shard_map.117 = (f32[256,512]{1,0:T(8,128)}, bf16[4,32,1024]{2,1,0:T(8,128)(2,1)}, f32[4,1,1152]{2,1,0:T(1,128)}) custom-call(bf16[2,4,256,512]{3,2,1,0:T(8,128)(2,1)} %pad_maximum_fusion.up, bf16[2,4,4,32,1024]{4,3,2,1,0:T(8,128)(2,1)} %pad_maximum_fusion.1.down, f32[2,1,1152]{2,1,0:T(1,128)} %pad_maximum_fusion.2.small), custom_call_target="tpu_custom_call" | custom-call | tf_op jit(solution)/shard_map/pallas_call | solution.py:299
  (84 shorter events, 17.1 us)
Async XLA Ops:
  0.6 2.8 %copy-start = (bf16[256,4096]{1,0:T(8,128)(2,1)S(1)}, bf16[256,4096]{1,0:T(8,128)(2,1)}, u32[]{:S(2)}) copy-start(bf16[256,4096]{1,0:T(8,128)(2,1)} %param.12) | copy-start | bytes 6291460
  0.6 2.5 %copy-start.18 = (s32[128,20]{0,1:T(8,128)S(1)}, s32[128,20]{0,1:T(8,128)}, u32[]{:S(2)}) copy-start(s32[128,20]{0,1:T(8,128)} %param.10) | copy-start | bytes 30724
  3.3 1.6 copy-start.12
  3.4 1.5 copy-start.16
  42.4 2.8 %copy-start.19 = (f32[2,1,1024]{2,1,0:T(1,128)S(1)}, f32[2,1,1024]{2,1,0:T(1,128)}, u32[]{:S(2)}) copy-start(f32[2,1,1024]{2,1,0:T(1,128)} %get-tuple-element.25) | copy-start | bytes 24580
  42.5 2.8 %copy-start.7 = (bf16[4,64,1024]{2,1,0:T(8,128)(2,1)S(1)}, bf16[4,64,1024]{2,1,0:T(8,128)(2,1)}, u32[]{:S(2)}) copy-start(bf16[4,64,1024]{2,1,0:T(8,128)(2,1)} %get-tuple-element.24) | copy-start | bytes 1572868
  65.0 2.8 %copy-start.8 = (bf16[4,64,1024]{2,1,0:T(8,128)(2,1)S(1)}, bf16[4,64,1024]{2,1,0:T(8,128)(2,1)}, u32[]{:S(2)}) copy-start(bf16[4,64,1024]{2,1,0:T(8,128)(2,1)} %get-tuple-element.24) | copy-start | bytes 1572868
  65.1 2.8 %copy-start.13 = (bf16[4,64,512]{2,1,0:T(8,128)(2,1)S(1)}, bf16[4,64,512]{2,1,0:T(8,128)(2,1)}, u32[]{:S(2)}) copy-start(bf16[4,64,512]{2,1,0:T(8,128)(2,1)} %get-tuple-element.28) | copy-start | bytes 786436
  67.9 3.0 %copy-start.3 = (bf16[1,4,4,32,1024]{4,3,2,1,0:T(8,128)(2,1)}, bf16[1,4,4,32,1024]{4,3,2,1,0:T(8,128)(2,1)S(1)}, u32[]{:S(2)}) copy-start(bf16[1,4,4,32,1024]{4,3,2,1,0:T(8,128)(2,1)S(1)} %get-tuple-element.45) | copy-start | bytes 3145732
  67.9 1.8 copy-start.9
  68.4 2.4 %copy-start.24 = (bf16[256,1024]{1,0:T(8,128)(2,1)}, bf16[256,1024]{1,0:T(8,128)(2,1)S(1)}, u32[]{:S(2)}) copy-start(bf16[256,1024]{1,0:T(8,128)(2,1)S(1)} %get-tuple-element.55) | copy-start | bytes 1572868
  69.7 20.6 %copy-start.23 = (s32[128]{0:T(128)S(1)}, s32[128]{0:T(128)}, u32[]{:S(2)}) copy-start(s32[128]{0:T(128)} %param.11) | copy-start | bytes 1540
  90.3 40.0 %copy-start.21 = (f32[4,1,64]{2,1,0:T(1,128)S(1)}, f32[4,1,64]{2,1,0:T(1,128)}, u32[]{:S(2)}) copy-start(f32[4,1,64]{2,1,0:T(1,128)} %get-tuple-element.35) | copy-start | bytes 3076
  135.1 2.3 %copy-start.4 = (bf16[1,4,4,32,1024]{4,3,2,1,0:T(8,128)(2,1)S(1)}, bf16[1,4,4,32,1024]{4,3,2,1,0:T(8,128)(2,1)}, u32[]{:S(2)}) copy-start(bf16[1,4,4,32,1024]{4,3,2,1,0:T(8,128)(2,1)} %copy-done.3) | copy-start | bytes 3145732
  137.4 1.2 copy-start.5
  137.4 16.8 %copy-start.20 = (f32[4,1,64]{2,1,0:T(1,128)S(1)}, f32[4,1,64]{2,1,0:T(1,128)}, u32[]{:S(2)}) copy-start(f32[4,1,64]{2,1,0:T(1,128)} %get-tuple-element.27) | copy-start | bytes 3076
  154.2 1.8 copy-start.10
  156.0 1.5 copy-start.2
  156.0 1.5 copy-start.14
  156.0 2.0 %copy-start.6 = (bf16[256,1024]{1,0:T(8,128)(2,1)S(1)}, bf16[256,1024]{1,0:T(8,128)(2,1)}, u32[]{:S(2)}) copy-start(bf16[256,1024]{1,0:T(8,128)(2,1)} %copy-done.5) | copy-start | bytes 1572868
  158.5 3.4 %copy-start.15 = (bf16[4,64,512]{2,1,0:T(8,128)(2,1)S(1)}, bf16[4,64,512]{2,1,0:T(8,128)(2,1)}, u32[]{:S(2)}) copy-start(bf16[4,64,512]{2,1,0:T(8,128)(2,1)} %get-tuple-element.39) | copy-start | bytes 786436
  160.0 2.5 %copy-start.22 = (f32[1,128]{1,0:T(1,128)S(1)}, f32[1,128]{1,0:T(1,128)}, u32[]{:S(2)}) copy-start(f32[1,128]{1,0:T(1,128)} %get-tuple-element.40) | copy-start | bytes 1540
  193.7 2.6 %copy-start.17 = (f32[4,1,1152]{2,1,0:T(1,128)S(1)}, f32[4,1,1152]{2,1,0:T(1,128)}, u32[]{:S(2)}) copy-start(f32[4,1,1152]{2,1,0:T(1,128)} %get-tuple-element.43) | copy-start | bytes 55300
  193.7 3.8 %copy-start.11 = (f32[256,512]{1,0:T(8,128)S(1)}, f32[256,512]{1,0:T(8,128)}, u32[]{:S(2)}) copy-start(f32[256,512]{1,0:T(8,128)} %get-tuple-element.41) | copy-start | bytes 1572868
  (1 other events, 0.8 us)
where the time goes:
time: 200 us; the launch traced here: 198 us
  Pallas kernels  149 us (74%)
  matrix products  20.8 us (10%)
  local copies, waits for them, and re-layouts  16.9 us (8%)
  other arithmetic  10.1 us (5%)
    pallas_call x7, Pallas kernels, call(): pl.pallas_call(kernel, out_shape=[jax.ShapeDtypeStruct(shape, kind) for s...  149 us
    dot_general x5, matrix products, contract_last(): lax.dot_general(left, right, (((1,), (1,)), ((), ())), preferred_element_...  9.24 us
    dot_general x6, matrix products, dot(): return jnp.dot(left, right, preferred_element_type=f32)  6.25 us
    dot_general x4, matrix products, contract_first(): lax.dot_general(left, right, (((0,), (0,)), ((), ())), preferred_element_...  5.33 us

commit v1 on v0

v1 whole, which is shorter than its diff:
```python
import functools
import math

import jax
import jax.numpy as jnp
from jax import lax
from jax.experimental import pallas as pl
from jax.experimental.pallas import tpu as pltpu
from jax.sharding import PartitionSpec as P

ROWS_DEV = 128
epsilon = 1e-06
logit_cap = 15.0
bf16 = jnp.bfloat16
f32 = jnp.float32
i32 = jnp.int32


def contract_last(left, right):
    return lax.dot_general(left, right, (((1,), (1,)), ((), ())), preferred_element_type=f32)


def contract_first(left, right):
    return lax.dot_general(left, right, (((0,), (0,)), ((), ())), preferred_element_type=f32)


def dot(left, right):
    return jnp.dot(left, right, preferred_element_type=f32)


def spread(rows, column, axis):
    here = lax.broadcasted_iota(i32, (rows, rows), 0)
    there = lax.broadcasted_iota(i32, (rows, rows), 1)
    wide = jnp.broadcast_to(column, (rows, rows))
    return jnp.sum(jnp.where(here == there, wide, 0.0), axis, keepdims=True)


def local(source, dest, sem):
    made = pltpu.make_async_copy(source, dest, sem)
    made.start()
    return made


def arrive(dest, sem):
    pltpu.make_async_copy(dest, dest, sem).wait()


def push(source, dest, sems, dp, section):
    made = pltpu.make_async_remote_copy(
        src_ref=source,
        dst_ref=dest,
        send_sem=sems[0],
        recv_sem=sems[1],
        device_id={"dp": dp, "section": section},
        device_id_type=pl.DeviceIdType.MESH,
    )
    made.start()
    return made


class Dims:
    def __init__(self, sections, devices, held, width, ff, vocab, samples, up_held, ff_held):
        self.sections, self.devices, self.held, self.width = sections, devices, held, width
        self.ff, self.vocab, self.samples = ff, vocab, samples
        self.up_held, self.ff_held = up_held, ff_held
        self.outer = 2 * sections
        self.inner = devices // self.outer
        self.cut = width // self.outer
        self.group = 2 * held
        self.part = self.group // sections


def scratch_of(d):
    S, O, I, E = d.sections, d.outer, d.inner, 2 * d.sections + 1
    V, D = pltpu.VMEM, pltpu.SemaphoreType.DMA
    part, cut, ff, held = d.part, d.cut, d.ff, d.held
    return dict(
        rep=V((2, held, cut), bf16),
        tab=V((2, d.vocab, cut), bf16),
        gains=V((S, 1, cut), f32),
        ups=V((S, I, d.up_held, ff), bf16),
        downs=V((S, O, I, d.ff_held, cut), bf16),
        away=V((held, cut), bf16),
        states=V((S + 1, d.group, cut), bf16),
        ready=V((S, d.group, cut), bf16),
        picks=V((2, held, d.samples), i32),
        marks=V((2, held, 1), i32),
        mine_marks=V((held, 1), i32),
        counts=V((part, d.vocab), f32),
        hots=V((part, d.vocab), f32),
        acc=V((S, part, ff), f32),
        cuts=V((2 * S, S, part, ff), bf16),
        got=V((2 * S, S, part, ff), bf16),
        swap=V((2 * S, 2, part, ff), bf16),
        score_cuts=V((S, part, d.vocab), f32),
        score_got=V((S, part, d.vocab), f32),
        score_swap=V((2, part, d.vocab), f32),
        stat_cuts=V((S, S, 1, part), f32),
        stat_got=V((S, S, 1, part), f32),
        stat_swap=V((S, 2, 1, part), f32),
        uppers=V((S, part, ff), f32),
        recips=V((S, part, 1), f32),
        actives=V((S, S, part, ff), bf16),
        d_all=V((S, part, d.vocab), bf16),
        d_uppers=V((S, S, part, ff), bf16),
        pulls=V((S, S, 1, part), f32),
        grad=V((d.group, cut), bf16),
        g_up=V((S, I, d.up_held, ff), bf16),
        g_down=V((S, O, I, d.ff_held, cut), bf16),
        up_in=V((S, I - 1, d.up_held, ff), bf16),
        down_in=V((S, I - 1, O, d.ff_held, cut), bf16),
        up_sum=V((S, d.up_held, ff), bf16),
        down_sum=V((S, O, d.ff_held, cut), bf16),
        up_end=V((S, d.up_held, ff), bf16),
        down_end=V((S, O, d.ff_held, cut), bf16),
        small=V((S, 1, cut + 128), f32),
        small_in=V((S, I - 1, 1, cut + 128), f32),
        small_sum=V((S, 1, cut + 128), f32),
        small_end=V((S, O, 1, cut + 128), f32),
        load_sems=D((4,)),
        gain_sems=D((2, S)),
        start_sems=D((3, 2)),
        col_up=D((2, S)),
        col_down=D((2, S, O)),
        send_down=D((O, S)),
        square=D((2, 2, S, I)),
        trade=D((2, E, 3, S)),
        stats=D((2, E, 3, S)),
        fold=D((2, 3, S, I)),
        end_up=D((2, S)),
        end_down=D((2, O, S)),
        end_small=D((2, O, S)),
    )


def step_kernel(d, names, *refs):
    ins, outs, held_refs = refs[:8], refs[8:12], refs[12:]
    replay, table, ids, sampled, targets, gain, up, down = ins
    grad_up, grad_down, grad_gain, loss = outs
    m = dict(zip(names, held_refs))
    S, O, I, W, R, FF, V = d.sections, d.outer, d.inner, d.cut, d.held, d.ff, d.vocab
    GS, G = d.part, d.group
    scale = math.sqrt(d.width)
    c = lax.axis_index("section")
    pos = lax.axis_index("dp")
    z, j = lax.div(pos, I), lax.rem(pos, I)
    zh, p = lax.div(z, 2), lax.rem(z, 2)
    q = 2 * c + p
    partner = (z + 1 - 2 * p) * I + j
    ups, downs, states, ready = m["ups"], m["downs"], m["states"], m["ready"]
    pending = []

    def column(k):
        return lax.rem(z + k, O) * I + j

    def section(k):
        return lax.rem(c + k, S)

    def square(k):
        return lax.rem(j + k, I)

    def pair(name, *at):
        return m[name].at[(0, *at)], m[name].at[(1, *at)]

    def send(source, dest, sems, dp, to):
        made = push(source, dest, sems, dp, to)
        pending.append(made.wait_send)
        return made

    def deliver(mine, source, dest, sems, dp, to):
        @pl.when(mine)
        def _():
            local(source, dest, sems[1])

        @pl.when(jnp.logical_not(mine))
        def _():
            push(source, dest, sems, dp, to)

        def finish():
            @pl.when(jnp.logical_not(mine))
            def _():
                arrive(source, sems[0])

        pending.append(finish)

    def cut_of(n):
        return pl.ds(pl.multiple_of(n * W, W), W)

    other = 2 * c + 1 - p
    loads = []
    for n, at in ((0, other), (1, q)):
        loads.append(local(replay.at[:, cut_of(at)], m["rep"].at[n], m["load_sems"].at[n]))
        loads.append(local(table.at[:, cut_of(at)], m["tab"].at[n], m["load_sems"].at[2 + n]))

    barrier = pltpu.get_barrier_semaphore()
    peers = [(column(a), section(b)) for a in range(O) for b in range(S) if a or b]
    peers += [(z * I + square(k), c) for k in range(1, I)]
    for dp, to in peers:
        pl.semaphore_signal(
            barrier, inc=1, device_id={"dp": dp, "section": to}, device_id_type=pl.DeviceIdType.MESH
        )
    pl.semaphore_wait(barrier, len(peers))

    for k in range(S):
        home = (2 * lax.rem(zh + k, S) + p) * I + j
        sems = (m["col_up"].at[0, k], m["col_up"].at[1, c])
        if k == 0:
            deliver(c == zh, up, ups.at[c, j], sems, home, zh)
        else:
            send(up, ups.at[c, j], sems, home, zh)
    for a in range(O):
        for b in range(S):
            there = lax.rem(z + a, O)
            piece = down.at[:, cut_of(2 * section(b) + lax.rem(there, 2))]
            dest = downs.at[c, z, j]
            if a or b:
                sems = (m["send_down"].at[a, b], m["col_down"].at[1, c, a])
                send(piece, dest, sems, column(a), section(b))
            else:
                local(piece, dest, m["col_down"].at[1, c, 0])
    for k in range(1, S):
        sems = pair("gain_sems", k)
        send(gain.at[:, cut_of(2 * section(k) + p)], m["gains"].at[c], sems, pos, section(k))
    local(gain.at[:, cut_of(q)], m["gains"].at[c], m["gain_sems"].at[1, 0])

    m["mine_marks"][...] = spread(R, targets[...].astype(f32), 1).astype(i32)
    m["marks"][p] = m["mine_marks"][...]
    m["picks"][p] = sampled[...]
    extra = [
        send(sampled, m["picks"].at[p], (m["start_sems"].at[0, 0], m["start_sems"].at[0, 1]), partner, c),
        send(m["mine_marks"], m["marks"].at[p], (m["start_sems"].at[1, 0], m["start_sems"].at[1, 1]), partner, c),
    ]
    id_hot = (lax.broadcasted_iota(i32, (R, R), 0) == ids[...] - pos * R).astype(bf16)
    taken = (lax.broadcasted_iota(i32, (R, V), 1) == sampled[:, 0:1]).astype(bf16)
    for n in range(2):
        loads[2 * n].wait()
        loads[2 * n + 1].wait()
        start = (contract_first(id_hot, m["rep"][n]) + dot(taken, m["tab"][n])).astype(bf16)
        mine_rows = pl.ds(pl.multiple_of(p * R, R), R)
        if n == 0:
            m["away"][...] = start
            sems = (m["start_sems"].at[2, 0], m["start_sems"].at[2, 1])
            moved = send(m["away"], states.at[0, mine_rows], sems, partner, c)
        else:
            states[0, mine_rows] = start

    for got in extra:
        got.wait_recv()
    first_row = c * GS
    chip, row = lax.div(first_row, R), pl.multiple_of(lax.rem(first_row, R), GS)
    picks = m["picks"][chip, pl.ds(row, GS)]
    marks = m["marks"][chip, pl.ds(row, GS)]
    actions = lax.broadcasted_iota(i32, (GS, V), 1)
    counts, hots = jnp.zeros((GS, V), f32), jnp.zeros((GS, V), f32)
    for k in range(d.samples):
        hit = jnp.where(picks[:, k : k + 1] == actions, 1.0, 0.0)
        counts += hit
        hots += jnp.where(marks == k, hit, 0.0)
    m["counts"][...] = counts
    m["hots"][...] = hots

    fans = {}

    def fan_up(layer):
        arrive(ups.at[layer, j], m["col_up"].at[1, layer])
        fans[0, layer] = [
            send(ups.at[layer, j], ups.at[layer, j], pair("square", 0, layer, k), z * I + square(k), c)
            for k in range(1, I)
        ]

    def fan_down(layer):
        for a in range(O):
            giver = lax.rem(z + O - a, O)
            arrive(downs.at[layer, giver, j], m["col_down"].at[1, layer, a])
        mine = downs.at[layer, :, j]
        fans[1, layer] = [
            send(mine, mine, pair("square", 1, layer, k), z * I + square(k), c) for k in range(1, I)
        ]

    def land(made):
        for copy in made:
            copy.wait_recv()

    def trade(e, partial, cuts, got, swap, stat=None, slot=None):
        m_acc = m["acc"]
        span = partial.shape[1]
        split = partial.reshape(S, GS, span)
        m_acc[:, :, :span] = split
        cuts[...] = split.astype(cuts.dtype)
        sent = [
            send(cuts.at[section(k)], got.at[k], pair("trade", e, 0, k), pos, section(k))
            for k in range(1, S)
        ]
        rows = []
        if stat is not None:
            for k in range(S):
                m["stat_cuts"][slot, k] = spread(GS, stat[k * GS : (k + 1) * GS], 0)
            rows = [
                send(
                    m["stat_cuts"].at[slot, section(k)],
                    m["stat_got"].at[slot, k],
                    pair("stats", e, 0, k),
                    pos,
                    section(k),
                )
                for k in range(1, S)
            ]

        def finish():
            land(sent)
            total = m_acc[c, :, :span]
            for k in range(1, S):
                total += got[k].astype(f32)
            swap[0] = total.astype(swap.dtype)
            over = send(swap.at[0], swap.at[1], pair("trade", e, 1, 0), partner, c)
            if stat is not None:
                land(rows)
                square_sum = m["stat_cuts"][slot, c]
                for k in range(1, S):
                    square_sum += m["stat_got"][slot, k]
                m["stat_swap"][slot, 0] = square_sum
                over_row = send(
                    m["stat_swap"].at[slot, 0],
                    m["stat_swap"].at[slot, 1],
                    pair("stats", e, 1, 0),
                    partner,
                    c,
                )

            def end():
                squares = None
                if stat is not None:
                    over_row.wait_recv()
                    squares = spread(GS, square_sum + m["stat_swap"][slot, 1], 1)
                over.wait_recv()
                return total + swap[1].astype(f32), squares

            return end

        return finish

    def gather(e, held):
        return [
            send(held.at[c], held.at[c], pair("trade", e, 2, k), pos, section(k))
            for k in range(1, S)
        ]

    for layer in range(S):
        fan_up(layer)
        fan_down(layer)
    moved.wait_recv()
    arrive(m["gains"].at[c], m["gain_sems"].at[1, 0])
    for k in range(1, S):
        giver = lax.rem(c + S - k, S)
        arrive(m["gains"].at[giver], m["gain_sems"].at[1, k])

    def ups_of(layer):
        return ups[layer].reshape(W, FF)

    def downs_of(layer):
        return downs[layer].reshape(FF, W)

    for layer in range(S):
        wide = states[layer].astype(f32)
        ready[layer] = (wide * m["gains"][layer]).astype(bf16)
        stat = jnp.sum(wide * wide, -1, keepdims=True)
        land(fans[0, layer])
        partial = dot(ready[layer], ups_of(layer))
        middle = trade(layer, partial, m["cuts"].at[layer], m["got"].at[layer], m["swap"].at[layer], stat, layer)
        total, squares = middle()()
        factor = lax.rsqrt(squares / d.width + epsilon)
        value = total * factor
        m["uppers"][layer] = value
        m["recips"][layer] = factor
        held = m["actives"].at[layer]
        held[c] = (value * jax.nn.sigmoid(value)).astype(bf16)
        moving = gather(layer, held)
        land(fans[1, layer])
        land(moving)
        states[layer + 1] = (
            states[layer].astype(f32) + dot(m["actives"][layer].reshape(G, FF), downs_of(layer))
        ).astype(bf16)

    part = contract_last(states[S], m["tab"][1])
    total, _ = trade(S, part, m["score_cuts"], m["score_got"], m["score_swap"])()()
    bent = jnp.tanh(total / scale / logit_cap)
    logits = logit_cap * bent
    counts, hots = m["counts"][...], m["hots"][...]
    weighted = counts * jnp.exp(logits)
    summed = jnp.sum(weighted, -1, keepdims=True)
    d_scores = (weighted / summed - hots) / ROWS_DEV * (1.0 - bent * bent) / scale
    m["d_all"][c] = d_scores.astype(bf16)
    moving = gather(S, m["d_all"])
    cross = jnp.log(summed) - jnp.sum(logits * hots, -1, keepdims=True)
    counted = jnp.where(p == 0, 1.0 / ROWS_DEV, 0.0)
    loss_here = jnp.broadcast_to(jnp.sum(cross, 0, keepdims=True) * counted, (1, 128))
    land(moving)
    m["grad"][...] = dot(m["d_all"][...].reshape(G, V), m["tab"][1]).astype(bf16)

    folds = {}

    def fold(kind, layer, source, dest):
        folds[kind, layer] = [
            send(source(square(k)), dest.at[layer, k - 1], pair("fold", kind, layer, k), z * I + square(k), c)
            for k in range(1, I)
        ]

    for layer in reversed(range(S)):
        e = S + 1 + layer
        slot = S + layer
        grad = m["grad"][...]
        part = contract_last(grad, downs_of(layer))
        middle = trade(e, part, m["cuts"].at[slot], m["got"].at[slot], m["swap"].at[slot])
        actives = m["actives"][layer].reshape(G, FF)
        end = middle()
        m["g_down"][layer] = contract_first(actives, grad).astype(bf16).reshape(O, I, d.ff_held, W)
        fold(1, layer, lambda at: m["g_down"].at[layer, :, at], m["down_in"])
        total, _ = end()
        value, factor = m["uppers"][layer], m["recips"][layer]
        sigm = jax.nn.sigmoid(value)
        d_upper = (total * sigm * (1.0 + value * (1.0 - sigm)) * factor).astype(bf16)
        held = m["d_uppers"].at[layer]
        held[c] = d_upper
        moving = gather(e, held)
        if layer:
            pull = jnp.sum(d_upper.astype(f32) * value, -1, keepdims=True) * factor / d.width
            m["pulls"][layer, c] = spread(GS, pull, 0)
            moving += [
                send(
                    m["pulls"].at[layer, c],
                    m["pulls"].at[layer, c],
                    pair("stats", e, 2, k),
                    pos,
                    section(k),
                )
                for k in range(1, S)
            ]
        land(moving)
        d_all = m["d_uppers"][layer].reshape(G, FF)
        wide = states[layer].astype(f32)
        d_normed = contract_last(d_all, ups_of(layer))
        m["small"][layer, :, :W] = jnp.sum(d_normed * wide, 0, keepdims=True)
        m["small"][layer, :, W:] = loss_here
        fold(2, layer, lambda at: m["small"].at[layer], m["small_in"])
        if layer:
            columns = jnp.concatenate([spread(GS, m["pulls"][layer, k], 1) for k in range(S)], 0)
            m["grad"][...] = (
                grad.astype(f32) + d_normed * m["gains"][layer] - wide * columns
            ).astype(bf16)
        m["g_up"][layer] = contract_first(ready[layer], d_all).astype(bf16).reshape(I, d.up_held, FF)
        fold(0, layer, lambda at: m["g_up"].at[layer, at], m["up_in"])

    home = q * I + j
    for layer in reversed(range(S)):
        land(folds[1, layer])
        value = m["g_down"][layer, :, j].astype(f32)
        for k in range(1, I):
            value += m["down_in"][layer, k - 1].astype(f32)
        m["down_sum"][layer] = value.astype(bf16)
        for a in range(O):
            there = lax.rem(z + a, O)
            source, dest = m["down_sum"].at[layer, there], m["down_end"].at[zh, q]
            sems = (m["end_down"].at[0, a, layer], m["end_down"].at[1, a, c])
            if a:
                send(source, dest, sems, column(a), layer)
            else:
                deliver(c == layer, source, dest, sems, pos, layer)
        land(folds[2, layer])
        value = m["small"][layer]
        for k in range(1, I):
            value += m["small_in"][layer, k - 1]
        m["small_sum"][layer] = value
        for a in range(O):
            source, dest = m["small_sum"].at[layer], m["small_end"].at[zh, q]
            sems = (m["end_small"].at[0, a, layer], m["end_small"].at[1, a, c])
            if a:
                send(source, dest, sems, column(a), layer)
            else:
                deliver(c == layer, source, dest, sems, pos, layer)
        land(folds[0, layer])
        value = m["g_up"][layer, j].astype(f32)
        for k in range(1, I):
            value += m["up_in"][layer, k - 1].astype(f32)
        m["up_sum"][layer] = value.astype(bf16)
        sems = (m["end_up"].at[0, layer], m["end_up"].at[1, zh])
        mine = jnp.logical_and(c == zh, c == layer)
        deliver(mine, m["up_sum"].at[layer], m["up_end"].at[zh], sems, home, layer)

    for a in range(O):
        giver = lax.rem(z + O - a, O)
        for b in range(S):
            cut = 2 * b + lax.rem(giver, 2)
            arrive(m["down_end"].at[lax.div(giver, 2), cut], m["end_down"].at[1, a, b])
            arrive(m["small_end"].at[lax.div(giver, 2), cut], m["end_small"].at[1, a, b])
    lost = jnp.zeros((1, 128), f32)
    for cut in range(O):
        value = jnp.zeros((d.ff_held, W), f32)
        row = jnp.zeros((1, W), f32)
        for h in range(S):
            value += m["down_end"][h, cut].astype(f32)
            row += m["small_end"][h, cut, :, :W]
            lost += m["small_end"][h, cut, :, W:]
        grad_down[:, cut * W : (cut + 1) * W] = value
        grad_gain[:, cut * W : (cut + 1) * W] = row
    loss[...] = lost
    value = jnp.zeros((d.up_held, FF), f32)
    for h in range(S):
        arrive(m["up_end"].at[h], m["end_up"].at[1, h])
        value += m["up_end"][h].astype(f32)
    grad_up[...] = value
    for finish in pending:
        finish()


def on_device(replay, state_ids, sampled, targets, action_table, norm_gain, w_up, w_down):
    held, width = replay.shape
    d = Dims(
        lax.axis_size("section"),
        lax.axis_size("dp"),
        held,
        width,
        w_up.shape[2],
        action_table.shape[0],
        sampled.shape[1],
        w_up.shape[1],
        w_down.shape[1],
    )
    scratch = scratch_of(d)
    vmem = pl.BlockSpec(memory_space=pltpu.VMEM)
    hbm = pl.BlockSpec(memory_space=pl.ANY)
    outs = ((d.up_held, d.ff), (d.ff_held, width), (1, width), (1, 128))
    grad_up, grad_down, grad_gain, loss = pl.pallas_call(
        functools.partial(step_kernel, d, tuple(scratch)),
        out_shape=[jax.ShapeDtypeStruct(shape, f32) for shape in outs],
        in_specs=[hbm, hbm, vmem, vmem, vmem, vmem, vmem, vmem],
        out_specs=[vmem] * 4,
        scratch_shapes=list(scratch.values()),
        compiler_params=pltpu.CompilerParams(
            collective_id=0, has_side_effects=True, vmem_limit_bytes=60 * 1024 * 1024
        ),
    )(
        replay,
        action_table,
        state_ids[None, :],
        sampled,
        targets[None, :],
        norm_gain,
        w_up[0],
        w_down[0],
    )
    return (grad_up[None], grad_down[None], grad_gain, loss[0, 0])


def solution(mesh):
    return jax.shard_map(
        on_device,
        mesh=mesh,
        in_specs=(
            P("dp", None),
            P("dp"),
            P("dp", None),
            P("dp"),
            P(),
            P("section", None),
            P("section", "dp", None),
            P("section", "dp", None),
        ),
        out_specs=(P("section", "dp", None), P("section", "dp", None), P("section", None), P()),
        check_vma=False,
    )
```

time: 200 us -> 148 us (0.74)
  matrix products: 20.8 us -> 0 us
  local copies, waits for them, and re-layouts: 16.9 us -> 5.79 us
  other arithmetic: 10.1 us -> 0 us
  Pallas kernels: 149 us -> 140 us
    dot_general x15 -> x0, matrix products: 20.8 us -> none  [the longest x5 9.24 us: contract_last(): lax.dot_general(left, right, (((1,), (1,)), ((), ())), preferred_element_...]
    pallas_call x7 -> x1, Pallas kernels: 149 us -> 140 us  [on_device(): pl.pallas_call(functools.partial(step_kernel, d, tuple(scratch)), out_sha...]
    slice x5 -> x0, local copies, waits for them, and re-layouts: 6.29 us -> none  [the longest x1 2.81 us: on_device(): state = (wide + dot(actives, downs[layer])).astype(bf16)]
    another operation x3 -> x0, other arithmetic: 3.03 us -> none  [the longest x1 1.51 us: on_device(): jnp.stack(grads_up[::-1]).reshape(sections, inner, up_held, ff)]
    unnamed x52 -> x8, local copies, waits for them, and re-layouts: 3.02 us -> 5.79 us
    pallas_call x3 -> x0, other arithmetic: 2.66 us -> none  [call(): pl.pallas_call(kernel, out_shape=[jax.ShapeDtypeStruct(shape, kind) for s...]
where the time goes in v1:
time: 148 us
  Pallas kernels  140 us (95%)
  local copies, waits for them, and re-layouts  5.79 us (4%)
  between operations  1.82 us (1%)
    pallas_call x1, Pallas kernels, on_device(): pl.pallas_call(functools.partial(step_kernel, d, tuple(scratch)), out_sha...  140 us
    unnamed x8, local copies, waits for them, and re-layouts  5.79 us

profile of v1, /device:TPU:0, one launch (start us, length us, event | category | flops | bytes accessed | tf_op | source)
XLA Modules:
  0.0 147.7 jit_solution(15367113861853224834)
XLA Ops:
  0.6 1.4 copy.12.refs_3_
  2.1 140.1 %shard_map.111 = (f32[256,512]{1,0:T(8,128)}, f32[32,4096]{1,0:T(8,128)}, f32[1,4096]{1,0:T(1,128)}, f32[1,128]{1,0:T(1,128)}) custom-call(bf16[128,4096]{1,0:T(8,128)(2,1)} %refs_0_.1, bf16[256,4096]{1,0:T(8,128)(2,1)} %refs_1_.1, s32[1,128]{1,0:T(1,128)} %bitcast.12, s32[128,20]{1,0:T(8,128)} %copy.12.refs_3_, s32[1,128]{1,0:T(1,128)} %bitcast.13, ...), custom_call_target="tpu_custom_call" | custom-call | tf_op jit(solution)/shard_map/pallas_call | solution.py:532
  142.2 0.0 copy-start
  142.2 0.0 copy-start.1
  142.2 1.9 %copy.17 = f32[1,256,512]{2,1,0:T(8,128)} copy(f32[1,256,512]{2,1,0:T(8,128)} %bitcast.9) | data formatting | bytes 1048576
  144.1 1.9 %copy.18 = f32[1,32,4096]{2,1,0:T(8,128)} copy(f32[1,32,4096]{2,1,0:T(8,128)} %bitcast.8) | data formatting | bytes 1048576
  145.9 0.0 copy-done
  145.9 0.6 copy.19
  146.5 0.0 copy-done.1
Async XLA Ops:
  142.2 3.8 %copy-start = (f32[1,4096]{1,0:T(1,128)S(1)}, f32[1,4096]{1,0:T(1,128)}, u32[]{:S(2)}) copy-start(f32[1,4096]{1,0:T(1,128)} %get-tuple-element.18) | copy-start | bytes 49156
  142.2 4.4 %copy-start.1 = (f32[1,128]{1,0:T(1,128)S(1)}, f32[1,128]{1,0:T(1,128)}, u32[]{:S(2)}) copy-start(f32[1,128]{1,0:T(1,128)} %get-tuple-element.11) | copy-start | bytes 1540

commit v2 on v1

v2 whole, which is shorter than its diff:
```python
import functools
import math
import types

import jax
import jax.numpy as jnp
from jax import lax
from jax.experimental import pallas as pl
from jax.experimental.pallas import tpu as pltpu
from jax.sharding import PartitionSpec as P

ROWS_DEV = 128
epsilon = 1e-06
logit_cap = 15.0
bf16 = jnp.bfloat16
f32 = jnp.float32
i32 = jnp.int32
DP, SECTION = "dp", "section"


def contract_last(left, right):
    return lax.dot_general(left, right, (((1,), (1,)), ((), ())), preferred_element_type=f32)


def contract_first(left, right):
    return lax.dot_general(left, right, (((0,), (0,)), ((), ())), preferred_element_type=f32)


def dot(left, right):
    return jnp.dot(left, right, preferred_element_type=f32)


def spread(rows, column, axis):
    here = lax.broadcasted_iota(i32, (rows, rows), 0)
    there = lax.broadcasted_iota(i32, (rows, rows), 1)
    wide = jnp.broadcast_to(column, (rows, rows))
    return jnp.sum(jnp.where(here == there, wide, 0.0), axis, keepdims=True)


def local(source, dest, sem):
    made = pltpu.make_async_copy(source, dest, sem)
    made.start()
    return made


def arrive(dest, sem):
    pltpu.make_async_copy(dest, dest, sem).wait()


def flip(j, k):
    low, high = lax.rem(j, 2), lax.div(j, 2)
    return (2 * (1 - high) if k & 2 else 2 * high) + ((1 - low) if k & 1 else low)


def push(source, dest, sems, dp, section):
    made = pltpu.make_async_remote_copy(
        src_ref=source,
        dst_ref=dest,
        send_sem=sems[0],
        recv_sem=sems[1],
        device_id={DP: dp, SECTION: section},
        device_id_type=pl.DeviceIdType.MESH,
    )
    made.start()
    return made


class Dims:
    def __init__(self, sections, devices, held, width, ff, vocab, samples, up_held, ff_held):
        self.sections, self.devices, self.held, self.width = sections, devices, held, width
        self.ff, self.vocab, self.samples = ff, vocab, samples
        self.up_held, self.ff_held = up_held, ff_held
        self.outer = 2 * sections
        self.inner = devices // self.outer
        self.cut = width // self.outer
        self.group = 2 * held
        self.part = self.group // sections
        self.factored = self.inner == 4 and self.up_held % 128 == 0


def scratch_of(d):
    S, O, I, E = d.sections, d.outer, d.inner, 2 * d.sections + 1
    V, D = pltpu.VMEM, pltpu.SemaphoreType.DMA
    part, cut, ff, held, others = d.part, d.cut, d.ff, d.held, max(S - 1, 1)
    if d.factored:
        kinds = dict(
            others=V((S, I, d.group, d.up_held), bf16),
            down_in=V((S, 6, O // 2, d.ff_held, cut), bf16),
            down_part=V((S, 2, O // 2, d.ff_held, cut), bf16),
            d_uppers=V((S, I, S, part, ff), bf16),
            other_sems=D((2, S)),
            upper_send=D((S,)),
            upper_recv=D((S, I - 1)),
            share_sems=D((2, S)),
            half_send=D((S,)),
            half_recv=D((S, 3)),
        )
    else:
        kinds = dict(
            g_up=V((S, I, d.up_held, ff), bf16),
            up_in=V((S, I - 1, d.up_held, ff), bf16),
            down_in=V((S, I - 1, O, d.ff_held, cut), bf16),
            d_uppers=V((S, 1, S, part, ff), bf16),
            fold=D((2, 2, S, I - 1)),
        )
    return dict(
        **kinds,
        rep=V((2, held, cut), bf16),
        tab=V((2, d.vocab, cut), bf16),
        gains=V((S, 1, cut), f32),
        ups=V((S, I, d.up_held, ff), bf16),
        downs=V((S, O, I, d.ff_held, cut), bf16),
        away=V((held, cut), bf16),
        states=V((S + 1, d.group, cut), bf16),
        ready=V((S, d.group, cut), bf16),
        picks=V((2, d.samples, held), i32),
        marks=V((2, 1, held), i32),
        counts=V((held, d.vocab), f32),
        hots=V((held, d.vocab), f32),
        acc=V((S, part, ff), f32),
        cuts=V((2 * S, S, part, ff), bf16),
        got=V((2 * S, S, part, ff), bf16),
        swap=V((2 * S, 2, part, ff), bf16),
        score_cuts=V((S, part, d.vocab), f32),
        score_got=V((S, part, d.vocab), f32),
        score_swap=V((2, part, d.vocab), f32),
        stat_cuts=V((S, S, 1, part), f32),
        stat_got=V((S, S, 1, part), f32),
        stat_swap=V((S, 2, 1, part), f32),
        uppers=V((S, part, ff), f32),
        recips=V((S, part, 1), f32),
        actives=V((S, S, part, ff), bf16),
        d_all=V((S, part, d.vocab), bf16),
        pulls=V((S, S, 1, part), f32),
        grad=V((d.group, cut), bf16),
        g_down=V((S, O, I, d.ff_held, cut), bf16),
        up_sum=V((S, d.up_held, ff), bf16),
        down_sum=V((S, O, d.ff_held, cut), bf16),
        up_end=V((S, d.up_held, ff), bf16),
        down_end=V((S, O, d.ff_held, cut), bf16),
        small=V((S, 1, cut + 128), f32),
        small_in=V((S, I - 1, 1, cut + 128), f32),
        small_sum=V((S, 1, cut + 128), f32),
        small_end=V((S, O, 1, cut + 128), f32),
        load_sems=D((4,)),
        gain_sems=D((2, S)),
        start_sems=D((3, 2)),
        col_up=D((2, S)),
        col_down=D((S,)),
        send_down=D((2,)),
        square_send=D((2, S)),
        square_recv=D((2, S, I - 1)),
        trade=D((2, E, 3, others)),
        tallies=D((2, S, 2, others)),
        pull_sems=D((2, S, others)),
        small_fold=D((2, S)),
        end_up=D((S,)),
        end_up_recv=D((1,)),
        end_down=D((2, S)),
        end_down_recv=D((1,)),
        end_small=D((2, S)),
        end_small_recv=D((1,)),
    )


def step_kernel(d, names, *refs):
    ins, outs, held_refs = refs[:8], refs[8:12], refs[12:]
    replay, table, ids, sampled, targets, gain, up, down = ins
    grad_up, grad_down, grad_gain, loss = outs
    m = types.SimpleNamespace(**dict(zip(names, held_refs)))
    S, O, I, W, R, FF, V = d.sections, d.outer, d.inner, d.cut, d.held, d.ff, d.vocab
    GS, G = d.part, d.group
    scale = math.sqrt(d.width)
    c = lax.axis_index(SECTION)
    pos = lax.axis_index(DP)
    z, j = lax.div(pos, I), lax.rem(pos, I)
    zh, p = lax.div(z, 2), lax.rem(z, 2)
    q = 2 * c + p
    partner = (z + 1 - 2 * p) * I + j
    ups, downs, states, ready = m.ups, m.downs, m.states, m.ready
    pending = []

    def column(k):
        return lax.rem(z + k, O) * I + j

    def section(k):
        return lax.rem(c + k, S)

    def square(k):
        return lax.rem(j + k, I)

    def pair(held, *at):
        return held.at[(0, *at)], held.at[(1, *at)]

    def send(source, dest, sems, dp, to, track=True):
        made = push(source, dest, sems, dp, to)
        if track:
            pending.append(made.wait_send)
        return made

    def settle(span, sem):
        pending.append(lambda: arrive(span, sem))

    def deliver(mine, source, dest, sems, dp, to, track=True):
        @pl.when(mine)
        def _():
            local(source, dest, sems[1])

        @pl.when(jnp.logical_not(mine))
        def _():
            push(source, dest, sems, dp, to)

        def finish():
            @pl.when(jnp.logical_not(mine))
            def _():
                arrive(source, sems[0])

        if track:
            pending.append(finish)

    def cut_of(n):
        return pl.ds(pl.multiple_of(n * W, W), W)

    other = 2 * c + 1 - p
    loads = []
    for n, at in ((0, other), (1, q)):
        loads.append(local(replay.at[:, cut_of(at)], m.rep.at[n], m.load_sems.at[n]))
        loads.append(local(table.at[:, cut_of(at)], m.tab.at[n], m.load_sems.at[2 + n]))

    barrier = pltpu.get_barrier_semaphore()
    peers = [(column(a), section(b)) for a in range(O) for b in range(S) if a or b]
    peers += [(z * I + square(k), c) for k in range(1, I)]
    for dp, to in peers:
        pl.semaphore_signal(
            barrier, inc=1, device_id={DP: dp, SECTION: to}, device_id_type=pl.DeviceIdType.MESH
        )
    pl.semaphore_wait(barrier, len(peers))

    def up_column():
        for k in range(S):
            home = (2 * lax.rem(zh + k, S) + p) * I + j
            sems = (m.col_up.at[0, k], m.col_up.at[1, c])
            if k == 0:
                deliver(c == zh, up, ups.at[c, j], sems, home, zh, False)
            else:
                push(up, ups.at[c, j], sems, home, zh)

    def down_column():
        for a in range(O):
            for b in range(S):
                there = lax.rem(z + a, O)
                piece = down.at[:, cut_of(2 * section(b) + lax.rem(there, 2))]
                dest = downs.at[c, z, j]
                if a or b:
                    sems = (m.send_down.at[0 if a else 1], m.col_down.at[c])
                    push(piece, dest, sems, column(a), section(b))
                else:
                    local(piece, dest, m.col_down.at[c])

    def drain_columns():
        @pl.when(c != zh)
        def _():
            arrive(up, m.col_up.at[0, 0])

        for k in range(1, S):
            arrive(up, m.col_up.at[0, k])
        arrive(downs.at[:, pl.ds(0, O - 1), 0], m.send_down.at[0])
        if S > 1:
            arrive(downs.at[pl.ds(0, S - 1), 0, 0], m.send_down.at[1])

    first = c == 0
    later = c != 0
    extra = [
        send(sampled, m.picks.at[p], (m.start_sems.at[0, 0], m.start_sems.at[0, 1]), partner, c),
        send(targets, m.marks.at[p], (m.start_sems.at[1, 0], m.start_sems.at[1, 1]), partner, c),
    ]

    @pl.when(first)
    def _():
        up_column()
        down_column()

    for k in range(1, S):
        sems = pair(m.gain_sems, k)
        send(gain.at[:, cut_of(2 * section(k) + p)], m.gains.at[c], sems, pos, section(k))
    local(gain.at[:, cut_of(q)], m.gains.at[c], m.gain_sems.at[1, 0])

    id_hot = (lax.broadcasted_iota(i32, (R, R), 0) == ids[...] - pos * R).astype(bf16)
    taken = (lax.broadcasted_iota(i32, (V, R), 0) == sampled[0:1]).astype(bf16)
    for n in range(2):
        loads[2 * n].wait()
        loads[2 * n + 1].wait()
        start = (contract_first(id_hot, m.rep[n]) + contract_first(taken, m.tab[n])).astype(bf16)
        mine_rows = pl.ds(pl.multiple_of(p * R, R), R)
        if n == 0:
            m.away[...] = start
            sems = (m.start_sems.at[2, 0], m.start_sems.at[2, 1])
            moved = send(m.away, states.at[0, mine_rows], sems, partner, c)
        else:
            states[0, mine_rows] = start

    chip, row = lax.div(c * GS, R), pl.multiple_of(lax.rem(c * GS, R), GS)

    def count():
        m.marks[p] = targets[...]
        m.picks[p] = sampled[...]
        land(extra)
        picks, marks = m.picks[chip], m.marks[chip]
        actions = lax.broadcasted_iota(i32, (V, R), 0)
        counts, hots = jnp.zeros((V, R), f32), jnp.zeros((V, R), f32)
        for k in range(d.samples):
            hit = jnp.where(picks[k : k + 1] == actions, 1.0, 0.0)
            counts += hit
            hots += jnp.where(marks == k, hit, 0.0)
        m.counts[...] = counts.T
        m.hots[...] = hots.T

    fans = {}
    relayed = I == 4

    def block(kind, layer, at, half=None):
        if kind == 0:
            if half is None:
                return ups.at[layer, at]
            return ups.at[layer, at, pl.ds(half * (d.up_held // 2), d.up_held // 2)]
        if half is None:
            return downs.at[layer, :, at]
        return downs.at[layer, pl.ds(half * (O // 2), O // 2), at]

    def blocks(kind, layer, n):
        return ups.at[layer, pl.ds(0, n)] if kind == 0 else downs.at[layer, :, pl.ds(0, n)]

    def fan(kind, layer):
        if kind == 0:
            arrive(ups.at[layer, j], m.col_up.at[1, layer])
        else:
            arrive(downs.at[layer, :, j], m.col_down.at[layer])
        going, coming = m.square_send.at[kind, layer], m.square_recv.at[kind, layer]
        made = fans[kind, layer] = {}
        if relayed:
            for k, half, n in ((1, 0, 0), (2, 1, 1), (1, 1, 2), (2, 0, 2)):
                view = block(kind, layer, j, half)
                to = z * I + flip(j, k)
                made[n] = send(view, view, (going, coming.at[n]), to, c, False)
        else:
            view = block(kind, layer, j)
            for k in range(1, I):
                to = z * I + square(k)
                made[k] = send(view, view, (going, coming.at[k - 1]), to, c, False)
        settle(blocks(kind, layer, I - 1), going)

    def relay(kind, layer):
        if relayed:
            made = fans[kind, layer]
            going, coming = m.square_send.at[kind, layer], m.square_recv.at[kind, layer]
            for k, half in ((1, 0), (2, 1)):
                land([made[half]])
                view = block(kind, layer, flip(j, k), half)
                send(view, view, (going, coming.at[2]), z * I + flip(j, 3 - k), c, False)

    def land_fan(kind, layer):
        if relayed:
            arrive(blocks(kind, layer, 2), m.square_recv.at[kind, layer, 2])
        else:
            land(fans[kind, layer])

    def land(made):
        for copy in made.values() if isinstance(made, dict) else made:
            copy.wait_recv()

    def tally(e, slot, stat):
        for k in range(S):
            m.stat_cuts[slot, k] = spread(GS, stat[k * GS : (k + 1) * GS], 0)
        rows = [
            send(
                m.stat_cuts.at[slot, section(k)],
                m.stat_got.at[slot, k],
                pair(m.tallies, slot, 0, k - 1),
                pos,
                section(k),
            )
            for k in range(1, S)
        ]

        def finish():
            land(rows)
            row = m.stat_cuts[slot, c]
            for k in range(1, S):
                row += m.stat_got[slot, k]
            m.stat_swap[slot, 0] = row
            swap = m.stat_swap.at[slot]
            over = send(swap.at[0], swap.at[1], pair(m.tallies, slot, 1, 0), partner, c)

            def end():
                land([over])
                return spread(GS, row + m.stat_swap[slot, 1], 1)

            return end

        return finish

    def trade(e, partial, cuts, got, swap):
        m_acc = m.acc
        span = partial.shape[1]
        split = partial.reshape(S, GS, span)
        m_acc[:, :, :span] = split
        cuts[...] = split.astype(cuts.dtype)
        sent = [
            send(cuts.at[section(k)], got.at[k], pair(m.trade, e, 0, k - 1), pos, section(k))
            for k in range(1, S)
        ]

        def finish():
            land(sent)
            total = m_acc[c, :, :span]
            for k in range(1, S):
                total += got[k].astype(f32)
            swap[0] = total.astype(swap.dtype)
            over = send(swap.at[0], swap.at[1], pair(m.trade, e, 1, 0), partner, c)

            def end():
                land([over])
                return total + swap[1].astype(f32)

            return end

        return finish

    def gather(e, held):
        return [
            send(held.at[c], held.at[c], pair(m.trade, e, 2, k - 1), pos, section(k))
            for k in range(1, S)
        ]

    fan(0, 0)
    count()
    relay(0, 0)
    fan(1, 0)
    pl.when(later)(up_column)
    moved.wait_recv()
    arrive(m.gains.at[c], m.gain_sems.at[1, 0])
    for k in range(1, S):
        giver = lax.rem(c + S - k, S)
        arrive(m.gains.at[giver], m.gain_sems.at[1, k])

    def lend(layer):
        if d.factored:
            own = pl.ds(pl.multiple_of(j * d.up_held, 128), d.up_held)
            m.others[layer, j] = ready[layer, :, own]
            for k in (1, 2, 3):
                send(
                    ready.at[layer, :, pl.ds(pl.multiple_of(flip(j, k) * d.up_held, 128), d.up_held)],
                    m.others.at[layer, j],
                    pair(m.other_sems, layer),
                    z * I + flip(j, k),
                    c,
                    False,
                )
            settle(m.others.at[layer, pl.ds(0, I - 1)], m.other_sems.at[0, layer])

    def ups_of(layer):
        return ups[layer].reshape(W, FF)

    def downs_of(layer):
        return downs[layer].reshape(FF, W)

    for layer in range(S):
        wide = states[layer].astype(f32)
        ready[layer] = (wide * m.gains[layer]).astype(bf16)
        counted = tally(layer, layer, jnp.sum(wide * wide, -1, keepdims=True))
        land_fan(0, layer)
        partial = dot(ready[layer], ups_of(layer))
        middle = trade(layer, partial, m.cuts.at[layer], m.got.at[layer], m.swap.at[layer])
        counted = counted()
        if layer == 0:
            pl.when(later)(down_column)
        relay(1, layer)
        if layer + 1 == S:
            for held_layer in range(S):
                lend(held_layer)
        end = middle()
        if layer + 1 < S:
            fan(0, layer + 1)
        factor = lax.rsqrt(counted() / d.width + epsilon)
        value = end() * factor
        m.uppers[layer] = value
        m.recips[layer] = factor
        held = m.actives.at[layer]
        held[c] = (value * jax.nn.sigmoid(value)).astype(bf16)
        moving = gather(layer, held)
        if layer + 1 < S:
            relay(0, layer + 1)
            fan(1, layer + 1)
        land_fan(1, layer)
        land(moving)
        states[layer + 1] = (
            states[layer].astype(f32) + dot(m.actives[layer].reshape(G, FF), downs_of(layer))
        ).astype(bf16)

    part = contract_last(states[S], m.tab[1])
    total = trade(S, part, m.score_cuts, m.score_got, m.score_swap)()()
    bent = jnp.tanh(total / scale / logit_cap)
    logits = logit_cap * bent
    counts, hots = m.counts[pl.ds(row, GS)], m.hots[pl.ds(row, GS)]
    weighted = counts * jnp.exp(logits)
    summed = jnp.sum(weighted, -1, keepdims=True)
    d_scores = (weighted / summed - hots) / ROWS_DEV * (1.0 - bent * bent) / scale
    m.d_all[c] = d_scores.astype(bf16)
    moving = gather(S, m.d_all)
    cross = jnp.log(summed) - jnp.sum(logits * hots, -1, keepdims=True)
    counted = jnp.where(p == 0, 1.0 / ROWS_DEV, 0.0)
    loss_here = jnp.broadcast_to(jnp.sum(cross, 0, keepdims=True) * counted, (1, 128))
    land(moving)
    m.grad[...] = dot(m.d_all[...].reshape(G, V), m.tab[1]).astype(bf16)

    folds = {}

    def fold(kind, layer, source, dest):
        folds[kind, layer] = [
            send(source(square(k)), dest.at[layer, k - 1], pair(m.fold, kind, layer, k - 1), z * I + square(k), c)
            for k in range(1, I)
        ]

    def fold_down(layer):
        if not d.factored:
            fold(1, layer, lambda at: m.g_down.at[layer, :, at], m.down_in)
            return
        made = folds[1, layer] = {}
        for n, k, at, half in ((1, 1, 3, 0), (3, 2, 3, 1), (0, 1, 1, 0), (2, 2, 2, 1)):
            source = m.g_down.at[layer, pl.ds(half * (O // 2), O // 2), flip(j, at)]
            sems = (m.half_send.at[layer], m.half_recv.at[layer, {1: 0, 3: 1}.get(n, 2)])
            made[n] = send(source, m.down_in.at[layer, n], sems, z * I + flip(j, k), c, False)

    def refold_down(layer):
        if not d.factored:
            return
        made = folds[1, layer]
        for n, k, half in ((1, 2, 0), (3, 1, 1)):
            land([made[n]])
            own = m.g_down[layer, half * (O // 2) : (half + 1) * (O // 2), flip(j, k)]
            into = m.down_part.at[layer, half]
            into[...] = (own.astype(f32) + m.down_in[layer, n].astype(f32)).astype(bf16)
            sems = (m.half_send.at[layer], m.half_recv.at[layer, 2])
            send(into, m.down_in.at[layer, 4 + half], sems, z * I + flip(j, k), c, False)
        settle(m.down_in.at[layer], m.half_send.at[layer])

    def down_total(layer):
        if not d.factored:
            land(folds[1, layer])
            value = m.g_down[layer, :, j].astype(f32)
            for k in range(1, I):
                value += m.down_in[layer, k - 1].astype(f32)
            m.down_sum[layer] = value.astype(bf16)
            return
        arrive(m.down_in.at[layer, pl.ds(0, 4)], m.half_recv.at[layer, 2])
        for half in range(2):
            rows = pl.ds(half * (O // 2), O // 2)
            value = m.g_down[layer, rows, j].astype(f32)
            for n in (2 * half, 4 + half):
                value += m.down_in[layer, n].astype(f32)
            m.down_sum[layer, rows] = value.astype(bf16)

    def share(layer):
        held = m.d_uppers.at[layer, j, c]
        folds[0, layer] = [
            (k, send(held, held, (m.upper_send.at[layer], m.upper_recv.at[layer, k - 1]), z * I + flip(j, k), c, False))
            for k in (1, 2, 3)
        ]
        settle(m.d_uppers.at[layer, pl.ds(0, I - 1), 0], m.upper_send.at[layer])

    def up_total(layer):
        if not d.factored:
            land(folds[0, layer])
            value = m.g_up[layer, j].astype(f32)
            for k in range(1, I):
                value += m.up_in[layer, k - 1].astype(f32)
            m.up_sum[layer] = value.astype(bf16)
            return
        for k, made in folds[0, layer]:
            land([made])
            held = m.d_uppers.at[layer, flip(j, k), c]
            for b in range(1, S):
                send(held, held, pair(m.share_sems, layer), pos, section(b), False)
        passed = m.d_uppers.at[layer, pl.ds(0, I - 1), pl.ds(0, S - 1)]
        settle(passed, m.share_sems.at[0, layer])
        arrive(m.others.at[layer, pl.ds(0, I - 1)], m.other_sems.at[1, layer])
        arrive(passed, m.share_sems.at[1, layer])
        value = contract_first(
            m.others[layer].reshape(I * G, d.up_held), m.d_uppers[layer].reshape(I * G, FF)
        )
        m.up_sum[layer] = value.astype(bf16)

    home = q * I + j

    def end_down(layer):
        down_total(layer)
        for a in range(O):
            there = lax.rem(z + a, O)
            source, dest = m.down_sum.at[layer, there], m.down_end.at[zh, q]
            sems = (m.end_down.at[0 if a else 1, layer], m.end_down_recv.at[0])
            if a:
                send(source, dest, sems, column(a), layer, False)
            else:
                deliver(c == layer, source, dest, sems, pos, layer)
        settle(m.down_end.at[0, pl.ds(0, O - 1)], m.end_down.at[0, layer])

    def end_small(layer):
        arrive(m.small_in.at[layer], m.small_fold.at[1, layer])
        value = m.small[layer]
        for k in range(1, I):
            value += m.small_in[layer, k - 1]
        m.small_sum[layer] = value
        for a in range(O):
            source, dest = m.small_sum.at[layer], m.small_end.at[zh, q]
            sems = (m.end_small.at[0 if a else 1, layer], m.end_small_recv.at[0])
            if a:
                send(source, dest, sems, column(a), layer, False)
            else:
                deliver(c == layer, source, dest, sems, pos, layer)
        settle(m.small_end.at[0, pl.ds(0, O - 1)], m.end_small.at[0, layer])

    def end_up(layer):
        up_total(layer)
        sems = (m.end_up.at[layer], m.end_up_recv.at[0])
        mine = jnp.logical_and(c == zh, c == layer)
        deliver(mine, m.up_sum.at[layer], m.up_end.at[zh], sems, home, layer)

    for layer in reversed(range(S)):
        e = S + 1 + layer
        slot = S + layer
        grad = m.grad[...]
        part = contract_last(grad, downs_of(layer))
        middle = trade(e, part, m.cuts.at[slot], m.got.at[slot], m.swap.at[slot])
        if layer + 1 < S:
            refold_down(layer + 1)
        end = middle()
        actives = m.actives[layer].reshape(G, FF)
        m.g_down[layer] = contract_first(actives, grad).astype(bf16).reshape(O, I, d.ff_held, W)
        fold_down(layer)
        if not layer:
            settled = pending[:]
            pending.clear()
        total = end()
        value, factor = m.uppers[layer], m.recips[layer]
        sigm = jax.nn.sigmoid(value)
        d_upper = (total * sigm * (1.0 + value * (1.0 - sigm)) * factor).astype(bf16)
        held = m.d_uppers.at[layer, j if d.factored else 0]
        held[c] = d_upper
        moving = gather(e, held)
        if layer and d.factored:
            share(layer)
        if layer:
            pull = jnp.sum(d_upper.astype(f32) * value, -1, keepdims=True) * factor / d.width
            m.pulls[layer, c] = spread(GS, pull, 0)
            moving += [
                send(
                    m.pulls.at[layer, c],
                    m.pulls.at[layer, c],
                    pair(m.pull_sems, layer, k - 1),
                    pos,
                    section(k),
                )
                for k in range(1, S)
            ]
        land(moving)
        d_all = held[...].reshape(G, FF)
        wide = states[layer].astype(f32)
        d_normed = contract_last(d_all, ups_of(layer))
        m.small[layer, :, :W] = jnp.sum(d_normed * wide, 0, keepdims=True)
        m.small[layer, :, W:] = loss_here
        if layer:
            columns = jnp.concatenate([spread(GS, m.pulls[layer, k], 1) for k in range(S)], 0)
            m.grad[...] = (
                grad.astype(f32) + d_normed * m.gains[layer] - wide * columns
            ).astype(bf16)
        for k in range(1, I):
            sems = pair(m.small_fold, layer)
            send(m.small.at[layer], m.small_in.at[layer, k - 1], sems, z * I + square(k), c, False)
        settle(m.small_in.at[layer], m.small_fold.at[0, layer])
        if not d.factored:
            m.g_up[layer] = contract_first(ready[layer], d_all).astype(bf16).reshape(I, d.up_held, FF)
            fold(0, layer, lambda at: m.g_up.at[layer, at], m.up_in)
        if layer + 1 < S:
            end_up(layer + 1)
            end_small(layer + 1)
            end_down(layer + 1)
    refold_down(0)
    if d.factored:
        share(0)
    drain_columns()
    for finish in settled:
        finish()
    end_down(0)
    end_small(0)
    end_up(0)
    arrive(m.small_end, m.end_small_recv.at[0])
    arrive(m.down_end, m.end_down_recv.at[0])
    lost = jnp.zeros((1, 128), f32)
    for cut in range(O):
        value = jnp.zeros((d.ff_held, W), f32)
        row = jnp.zeros((1, W), f32)
        for h in range(S):
            value += m.down_end[h, cut].astype(f32)
            row += m.small_end[h, cut, :, :W]
            lost += m.small_end[h, cut, :, W:]
        grad_down[:, cut * W : (cut + 1) * W] = value
        grad_gain[:, cut * W : (cut + 1) * W] = row
    loss[...] = lost
    for finish in pending:
        finish()
    value = jnp.zeros((d.up_held, FF), f32)
    arrive(m.up_end, m.end_up_recv.at[0])
    for h in range(S):
        value += m.up_end[h].astype(f32)
    grad_up[...] = value


def on_device(replay, state_ids, sampled, targets, action_table, norm_gain, w_up, w_down):
    held, width = replay.shape
    d = Dims(
        lax.axis_size(SECTION),
        lax.axis_size(DP),
        held,
        width,
        w_up.shape[2],
        action_table.shape[0],
        sampled.shape[1],
        w_up.shape[1],
        w_down.shape[1],
    )
    scratch = scratch_of(d)
    vmem = pl.BlockSpec(memory_space=pltpu.VMEM)
    hbm = pl.BlockSpec(memory_space=pltpu.HBM)
    outs = ((d.up_held, d.ff), (d.ff_held, width), (1, width), (1, 128))
    grad_up, grad_down, grad_gain, loss = pl.pallas_call(
        functools.partial(step_kernel, d, tuple(scratch)),
        out_shape=[jax.ShapeDtypeStruct(shape, f32) for shape in outs],
        in_specs=[hbm, hbm, vmem, vmem, vmem, vmem, vmem, vmem],
        out_specs=[vmem] * 4,
        scratch_shapes=list(scratch.values()),
        compiler_params=pltpu.CompilerParams(
            collective_id=0, has_side_effects=True, vmem_limit_bytes=48 * 1024 * 1024
        ),
    )(
        *(
            pltpu.with_memory_space_constraint(x, pltpu.HBM)
            for x in (
                replay,
                action_table,
                state_ids[None, :],
                sampled.T,
                targets[None, :],
                norm_gain,
                w_up[0],
                w_down[0],
            )
        )
    )
    return (grad_up[None], grad_down[None], grad_gain, loss[0, 0])


def solution(mesh):
    return jax.shard_map(
        on_device,
        mesh=mesh,
        in_specs=(
            P("dp", None),
            P("dp"),
            P("dp", None),
            P("dp"),
            P(),
            P("section", None),
            P("section", "dp", None),
            P("section", "dp", None),
        ),
        out_specs=(P("section", "dp", None), P("section", "dp", None), P("section", None), P()),
        check_vma=False,
    )
```

time: 148 us -> 105 us (0.71)
  Pallas kernels: 140 us -> 101 us
  local copies, waits for them, and re-layouts: 5.79 us -> 2.19 us
    pallas_call x1, Pallas kernels: 140 us -> 101 us  [on_device(): pl.pallas_call(functools.partial(step_kernel, d, tuple(scratch)), out_sha...]
    unnamed x8 -> x3, local copies, waits for them, and re-layouts: 5.79 us -> 2.19 us
where the time goes in v2:
time: 105 us
  Pallas kernels  101 us (96%)
  local copies, waits for them, and re-layouts  2.19 us (2%)
  between operations  1.81 us (2%)
    pallas_call x1, Pallas kernels, on_device(): pl.pallas_call(functools.partial(step_kernel, d, tuple(scratch)), out_sha...  101 us
    unnamed x3, local copies, waits for them, and re-layouts  2.19 us

profile of v2, /device:TPU:0, one launch (start us, length us, event | category | flops | bytes accessed | tf_op | source)
XLA Modules:
  0.0 105.0 jit_solution(15730333291173831747)
XLA Ops:
  0.6 101.0 %shard_map.111 = (f32[256,512]{1,0:T(8,128)S(1)}, f32[32,4096]{1,0:T(8,128)S(1)}, f32[1,4096]{1,0:T(1,128)S(1)}, f32[1,128]{1,0:T(1,128)S(1)}) custom-call(bf16[128,4096]{1,0:T(8,128)(2,1)} %refs_0_.1, bf16[256,4096]{1,0:T(8,128)(2,1)} %refs_1_.1, s32[1,128]{1,0:T(1,128)} %bitcast.15, s32[20,128]{1,0:T(8,128)} %bitcast.14, s32[1,128]{1,0:T(1,128)} %bitcast.16, ...), custom_call_target="tpu_custom_call" | custom-call | tf_op jit(solution)/shard_map/pallas_call | solution.py:735
  101.6 0.8 copy.16
  102.4 0.8 copy.17
  103.2 0.6 copy.18

commit v3 on v2

--- a/solution.py
+++ b/solution.py
@@ -123,7 +123,7 @@
         swap=V((2 * S, 2, part, ff), bf16),
         score_cuts=V((S, part, d.vocab), f32),
         score_got=V((S, part, d.vocab), f32),
-        score_swap=V((2, part, d.vocab), f32),
+        score_swap=V((2, part, d.vocab), bf16),
         stat_cuts=V((S, S, 1, part), f32),
         stat_got=V((S, S, 1, part), f32),
         stat_swap=V((S, 2, 1, part), f32),
@@ -136,12 +136,9 @@
         g_down=V((S, O, I, d.ff_held, cut), bf16),
         up_sum=V((S, d.up_held, ff), bf16),
         down_sum=V((S, O, d.ff_held, cut), bf16),
-        up_end=V((S, d.up_held, ff), bf16),
-        down_end=V((S, O, d.ff_held, cut), bf16),
         small=V((S, 1, cut + 128), f32),
         small_in=V((S, I - 1, 1, cut + 128), f32),
         small_sum=V((S, 1, cut + 128), f32),
-        small_end=V((S, O, 1, cut + 128), f32),
         load_sems=D((4,)),
         gain_sems=D((2, S)),
         start_sems=D((3, 2)),
@@ -164,10 +161,10 @@
 
 
 def step_kernel(d, names, *refs):
-    ins, outs, held_refs = refs[:8], refs[8:12], refs[12:]
+    ins, outs, held_refs = refs[:8], refs[8:11], refs[11:]
     replay, table, ids, sampled, targets, gain, up, down = ins
-    grad_up, grad_down, grad_gain, loss = outs
     m = types.SimpleNamespace(**dict(zip(names, held_refs)))
+    m.up_end, m.down_end, m.small_end = outs
     S, O, I, W, R, FF, V = d.sections, d.outer, d.inner, d.cut, d.held, d.ff, d.vocab
     GS, G = d.part, d.group
     scale = math.sqrt(d.width)
@@ -695,24 +692,29 @@
     end_up(0)
     arrive(m.small_end, m.end_small_recv.at[0])
     arrive(m.down_end, m.end_down_recv.at[0])
-    lost = jnp.zeros((1, 128), f32)
-    for cut in range(O):
-        value = jnp.zeros((d.ff_held, W), f32)
-        row = jnp.zeros((1, W), f32)
-        for h in range(S):
-            value += m.down_end[h, cut].astype(f32)
-            row += m.small_end[h, cut, :, :W]
-            lost += m.small_end[h, cut, :, W:]
-        grad_down[:, cut * W : (cut + 1) * W] = value
-        grad_gain[:, cut * W : (cut + 1) * W] = row
-    loss[...] = lost
     for finish in pending:
         finish()
-    value = jnp.zeros((d.up_held, FF), f32)
     arrive(m.up_end, m.end_up_recv.at[0])
-    for h in range(S):
-        value += m.up_end[h].astype(f32)
-    grad_up[...] = value
+
+
+def sum_kernel(d, up_end, down_end, small_end, grad_up, grad_down, grad_gain, loss):
+    W = d.cut
+
+    def total(pieces):
+        value = pieces[0].astype(f32)
+        for piece in pieces[1:]:
+            value += piece.astype(f32)
+        return value
+
+    groups = range(d.sections)
+    lost = []
+    grad_up[...] = total([up_end[h] for h in groups])
+    for cut in range(d.outer):
+        at = slice(cut * W, (cut + 1) * W)
+        grad_down[:, at] = total([down_end[h, cut] for h in groups])
+        grad_gain[:, at] = total([small_end[h, cut, :, :W] for h in groups])
+        lost += [small_end[h, cut, :, W:] for h in groups]
+    loss[0, 0] = total(lost)[0, 0]
 
 
 def on_device(replay, state_ids, sampled, targets, action_table, norm_gain, w_up, w_down):
@@ -731,12 +733,16 @@
     scratch = scratch_of(d)
     vmem = pl.BlockSpec(memory_space=pltpu.VMEM)
     hbm = pl.BlockSpec(memory_space=pltpu.HBM)
-    outs = ((d.up_held, d.ff), (d.ff_held, width), (1, width), (1, 128))
-    grad_up, grad_down, grad_gain, loss = pl.pallas_call(
+    ends = (
+        jax.ShapeDtypeStruct((d.sections, d.up_held, d.ff), bf16),
+        jax.ShapeDtypeStruct((d.sections, d.outer, d.ff_held, d.cut), bf16),
+        jax.ShapeDtypeStruct((d.sections, d.outer, 1, d.cut + 128), f32),
+    )
+    parts = pl.pallas_call(
         functools.partial(step_kernel, d, tuple(scratch)),
-        out_shape=[jax.ShapeDtypeStruct(shape, f32) for shape in outs],
+        out_shape=ends,
         in_specs=[hbm, hbm, vmem, vmem, vmem, vmem, vmem, vmem],
-        out_specs=[vmem] * 4,
+        out_specs=[vmem] * 3,
         scratch_shapes=list(scratch.values()),
         compiler_params=pltpu.CompilerParams(
             collective_id=0, has_side_effects=True, vmem_limit_bytes=48 * 1024 * 1024
@@ -756,7 +762,15 @@
             )
         )
     )
-    return (grad_up[None], grad_down[None], grad_gain, loss[0, 0])
+    outs = ((d.up_held, d.ff), (d.ff_held, width), (1, width), (1, 1))
+    grad_up, grad_down, grad_gain, loss = pl.pallas_call(
+        functools.partial(sum_kernel, d),
+        out_shape=[jax.ShapeDtypeStruct(shape, f32) for shape in outs],
+        in_specs=[vmem] * 3,
+        out_specs=[vmem] * 3 + [pl.BlockSpec(memory_space=pltpu.SMEM)],
+        compiler_params=pltpu.CompilerParams(vmem_limit_bytes=8 * 1024 * 1024),
+    )(*parts)
+    return (grad_up[None], grad_down[None], grad_gain, loss.reshape(()))
 
 
 def solution(mesh):

time: 105 us -> 102 us (0.971)
  local copies, waits for them, and re-layouts: 2.19 us -> 0 us
  between operations: 1.81 us -> 0.64 us
    unnamed x3 -> x0, local copies, waits for them, and re-layouts: 2.19 us -> none
    pallas_call x1, Pallas kernels: 101 us -> 99.6 us  [on_device(): pl.pallas_call(functools.partial(step_kernel, d, tuple(scratch)), out_sha...]
    pallas_call x0 -> x1, Pallas kernels: none -> 1.06 us  [on_device(): pl.pallas_call(functools.partial(sum_kernel, d), out_shape=[jax.ShapeDtyp...]
where the time goes in v3:
time: 102 us; the launch traced here: 101 us
  Pallas kernels  101 us (99%)
    pallas_call x1, Pallas kernels, on_device(): pl.pallas_call(functools.partial(step_kernel, d, tuple(scratch)), out_sha...  99.6 us

profile of v3, /device:TPU:0, one launch (start us, length us, event | category | flops | bytes accessed | tf_op | source)
XLA Modules:
  0.0 101.3 jit_solution(5347261042270165309)
XLA Ops:
  0.6 99.6 %shard_map.111 = (bf16[2,256,512]{2,1,0:T(8,128)(2,1)S(1)}, bf16[2,4,32,1024]{3,2,1,0:T(8,128)(2,1)S(1)}, f32[2,4,1,1152]{3,2,1,0:T(1,128)S(1)}) custom-call(bf16[128,4096]{1,0:T(8,128)(2,1)} %refs_0_.1, bf16[256,4096]{1,0:T(8,128)(2,1)} %refs_1_.1, s32[1,128]{1,0:T(1,128)} %bitcast.11, s32[20,128]{1,0:T(8,128)} %bitcast.10, s32[1,128]{1,0:T(1,128)} %bitcast.12, ...), custom_call_target="tpu_custom_call" | custom-call | tf_op jit(solution)/shard_map/pallas_call | solution.py:741
  100.2 1.1 %shard_map.112 = (f32[256,512]{1,0:T(8,128)}, f32[32,4096]{1,0:T(8,128)}, f32[1,4096]{1,0:T(1,128)}, f32[1,1]{1,0:T(1,128)}) custom-call(bf16[2,256,512]{2,1,0:T(8,128)(2,1)S(1)} %get-tuple-element.11.up_end, bf16[2,4,32,1024]{3,2,1,0:T(8,128)(2,1)S(1)} %get-tuple-element.12.down_end, f32[2,4,1,1152]{3,2,1,0:T(1,128)S(1)} %get-tuple-element.13.small_end), custom_call_target="tpu_custom_call" | custom-call | tf_op jit(solution)/shard_map/pallas_call | solution.py:766

commit v4 on v3

--- a/solution.py
+++ b/solution.py
@@ -105,6 +105,12 @@
         )
     return dict(
         **kinds,
+        ids=V((1, held), i32),
+        sampled=V((d.samples, held), i32),
+        targets=V((1, held), i32),
+        gain=V((1, d.width), f32),
+        up=V((d.up_held, ff), bf16),
+        down=V((d.ff_held, d.width), bf16),
         rep=V((2, held, cut), bf16),
         tab=V((2, d.vocab, cut), bf16),
         gains=V((S, 1, cut), f32),
@@ -140,6 +146,7 @@
         small_in=V((S, I - 1, 1, cut + 128), f32),
         small_sum=V((S, 1, cut + 128), f32),
         load_sems=D((4,)),
+        first_sems=D((6,)),
         gain_sems=D((2, S)),
         start_sems=D((3, 2)),
         col_up=D((2, S)),
@@ -162,9 +169,10 @@
 
 def step_kernel(d, names, *refs):
     ins, outs, held_refs = refs[:8], refs[8:11], refs[11:]
-    replay, table, ids, sampled, targets, gain, up, down = ins
+    replay, table, *firsts = ins
     m = types.SimpleNamespace(**dict(zip(names, held_refs)))
     m.up_end, m.down_end, m.small_end = outs
+    ids, sampled, targets, gain, up, down = kept = m.ids, m.sampled, m.targets, m.gain, m.up, m.down
     S, O, I, W, R, FF, V = d.sections, d.outer, d.inner, d.cut, d.held, d.ff, d.vocab
     GS, G = d.part, d.group
     scale = math.sqrt(d.width)
@@ -218,12 +226,6 @@
     def cut_of(n):
         return pl.ds(pl.multiple_of(n * W, W), W)
 
-    other = 2 * c + 1 - p
-    loads = []
-    for n, at in ((0, other), (1, q)):
-        loads.append(local(replay.at[:, cut_of(at)], m.rep.at[n], m.load_sems.at[n]))
-        loads.append(local(table.at[:, cut_of(at)], m.tab.at[n], m.load_sems.at[2 + n]))
-
     barrier = pltpu.get_barrier_semaphore()
     peers = [(column(a), section(b)) for a in range(O) for b in range(S) if a or b]
     peers += [(z * I + square(k), c) for k in range(1, I)]
@@ -231,7 +233,15 @@
         pl.semaphore_signal(
             barrier, inc=1, device_id={DP: dp, SECTION: to}, device_id_type=pl.DeviceIdType.MESH
         )
+    early = [local(firsts[n], kept[n], m.first_sems.at[n]) for n in (3, 2, 4, 5, 1, 0)]
+    other = 2 * c + 1 - p
+    loads = []
+    for n, at in ((0, other), (1, q)):
+        loads.append(local(replay.at[:, cut_of(at)], m.rep.at[n], m.load_sems.at[n]))
+        loads.append(local(table.at[:, cut_of(at)], m.tab.at[n], m.load_sems.at[2 + n]))
     pl.semaphore_wait(barrier, len(peers))
+    for copy in early:
+        copy.wait()
 
     def up_column():
         for k in range(S):
@@ -741,7 +751,7 @@
     parts = pl.pallas_call(
         functools.partial(step_kernel, d, tuple(scratch)),
         out_shape=ends,
-        in_specs=[hbm, hbm, vmem, vmem, vmem, vmem, vmem, vmem],
+        in_specs=[hbm] * 8,
         out_specs=[vmem] * 3,
         scratch_shapes=list(scratch.values()),
         compiler_params=pltpu.CompilerParams(

time: 102 us -> 100 us (0.980)
  Pallas kernels: 101 us -> 99.6 us
    pallas_call x1, Pallas kernels: 99.6 us -> 98.5 us  [on_device(): pl.pallas_call(functools.partial(step_kernel, d, tuple(scratch)), out_sha...]
where the time goes in v4:
time: 100 us
  Pallas kernels  99.6 us (100%)
    pallas_call x1, Pallas kernels, on_device(): pl.pallas_call(functools.partial(step_kernel, d, tuple(scratch)), out_sha...  98.5 us

profile of v4, /device:TPU:0, one launch (start us, length us, event | category | flops | bytes accessed | tf_op | source)
XLA Modules:
  0.0 100.2 jit_solution(9906796612123963158)
XLA Ops:
  0.6 98.5 %shard_map.111 = (bf16[2,256,512]{2,1,0:T(8,128)(2,1)S(1)}, bf16[2,4,32,1024]{3,2,1,0:T(8,128)(2,1)S(1)}, f32[2,4,1,1152]{3,2,1,0:T(1,128)S(1)}) custom-call(bf16[128,4096]{1,0:T(8,128)(2,1)} %refs_0_.1, bf16[256,4096]{1,0:T(8,128)(2,1)} %refs_1_.1, s32[1,128]{1,0:T(1,128)} %bitcast.11, s32[20,128]{1,0:T(8,128)} %bitcast.10, s32[1,128]{1,0:T(1,128)} %bitcast.12, ...), custom_call_target="tpu_custom_call" | custom-call | tf_op jit(solution)/shard_map/pallas_call | solution.py:751
  99.2 1.1 %shard_map.112 = (f32[256,512]{1,0:T(8,128)}, f32[32,4096]{1,0:T(8,128)}, f32[1,4096]{1,0:T(1,128)}, f32[1,1]{1,0:T(1,128)}) custom-call(bf16[2,256,512]{2,1,0:T(8,128)(2,1)S(1)} %get-tuple-element.11.up_end, bf16[2,4,32,1024]{3,2,1,0:T(8,128)(2,1)S(1)} %get-tuple-element.12.down_end, f32[2,4,1,1152]{3,2,1,0:T(1,128)S(1)} %get-tuple-element.13.small_end), custom_call_target="tpu_custom_call" | custom-call | tf_op jit(solution)/shard_map/pallas_call | solution.py:776
